TPU v7x, 256 devices: a whole 4x4x8 slice. The times are simulated.
256 devices in a mesh: grp: 8 (over y, core), dev: 32 (over x, z).
Axes of the slice: x: 4, y: 4, z: 8, core: 2. Of those that a mesh axis runs over, the one named last changes fastest.
Arguments:
- densities: bfloat16 [256, 200, 200], P(('grp', 'dev')), may hold values from -0.4375 to 0.4375
- core_hamiltonian: bfloat16 [256, 200, 200], P(('grp', 'dev')), may hold values from -0.21875 to 0.21875
- embedding: bfloat16 [256, 200, 200], P(('grp', 'dev')), may hold values from -0.21875 to 0.21875
- fit_factors: bfloat16 [768, 200, 200], P('dev'), may hold values from -0.059814453 to 0.059814453
- orthogonalizers: bfloat16 [256, 200, 200], P(('grp', 'dev'))
- pairs: int32 [3072, 2], replicated, may hold values from 0 to 255, as said below
- assignment: int32 [3072], replicated, may hold values from 0 to 31, as said below
- owner_map: int32 [256], replicated, may hold values from 0 to 255, as said below
Outputs:
- slot_energies: float32 [6144], P(('grp', 'dev'))
- total: float32 [], replicated
Inputs may be any that keep to these rules, and one draw needn't show every extreme that they name: `pairs`: dimer k belongs to group g = k // 384; its first fragment lies in block g, the fragments g * 32 to (g + 1) * 32 - 1, and its second fragment, different from the first, lies in block g or block g + 1 (only block g for the last group). `assignment`: no device receives more than 24 dimers of its group, and in every group some device receives exactly 24. `owner_map`: A permutation of the fragments that maps each block of 32 fragments onto the rows of the same block.
All inputs are finite; a program needn't handle non-finite values.
Results may differ from a plain program's by a relative error of at most 0.0003.
Values may be sent and summed in bfloat16 or wider, within the bound.
No kernel may reach another device: no remote copies, remote signals or barrier semaphores. Data moves between devices by JAX's collectives and lax.ppermute only.
A program may use at most 128 MiB of HBM per device.

v0:
```python
import functools

import jax
import jax.numpy as jnp
from jax import lax
from jax.experimental import pallas as pl
from jax.experimental.pallas import tpu as pltpu
from jax.sharding import Mesh
from jax.sharding import PartitionSpec as P

SLOTS = 24
LANES = 128
DEV = ("dev_0", "dev_1")
GRP_DEV = ("grp", "dev_0", "dev_1")
HALF_WIDTH = 4.0


def moved(block, axis, distance):
    count = lax.axis_size(axis)
    return lax.ppermute(block, axis, [(i, (i + distance) % count) for i in range(count)])


def from_behind(block, axis, distance):
    devices = range(lax.axis_size(axis))
    route = [(i - distance, i) for i in devices if i - distance in devices]
    return lax.ppermute(block, axis, route)


def along_ring(block, axis):
    half = lax.axis_size(axis) // 2
    behind, ahead = [block], [block]
    for _ in range(half - 1):
        behind.append(moved(behind[-1], axis, 1))
        ahead.append(moved(ahead[-1], axis, -1))
    cut = block.shape[0] // 2
    far = jnp.concatenate([moved(behind[-1][:cut], axis, 1), moved(ahead[-1][cut:], axis, -1)])
    return behind + [far] + ahead[:0:-1]


def along_line(block, axis):
    return [block] + [moved(block, axis, k) for k in range(1, lax.axis_size(axis))]


def summed_columns(terms, axis):
    cut = terms[0].shape[1] // 16 * 8 + 8
    low, high = [t[:, :cut] for t in terms], [t[:, cut:] for t in terms]
    passing_down = moved(low[2], axis, -1)
    passing_up = moved(high[2], axis, 1)
    high_down = moved(high[1], axis, -1)
    low_up = moved(low[3], axis, 1)
    low_down = moved(added(low[1], passing_down), axis, -1)
    high_up = moved(added(high[3], passing_up), axis, 1)
    return jnp.concatenate(
        [added(low[0], low_up, low_down), added(high[0], high_up, high_down)], axis=1
    )


def added(*arrays):
    return functools.reduce(jnp.add, [a.astype(jnp.float32) for a in arrays]).astype(jnp.bfloat16)


def coefficients(dens, fit_factors):
    return jnp.einsum("rmn,pmn->rp", dens, fit_factors, preferred_element_type=jnp.float32)


def exchanged(array, axis):
    return lax.all_to_all(array, axis, split_axis=0, concat_axis=0, tiled=True)


def sent_to_all(array, axis):
    copies = jnp.broadcast_to(array, (lax.axis_size(axis), *array.shape))
    return lax.all_to_all(copies, axis, split_axis=0, concat_axis=0, tiled=True)


def product(left, right):
    return jnp.dot(left, right, preferred_element_type=jnp.float32)


def turned(left, right):
    return lax.dot_general(
        left, right, (((0,), (0,)), ((), ())), preferred_element_type=jnp.float32
    )


def stage(function, *lists):
    return [function(*items) for items in zip(*lists)]


def dimer_terms(operands):
    size = operands[0][0].shape[0]
    low = jnp.bfloat16
    rows = lax.broadcasted_iota(jnp.int32, (size, size), 0)
    columns = lax.broadcasted_iota(jnp.int32, (size, size), 1)
    middle = jnp.where(rows == columns, 0.5, 0.0).astype(jnp.float32)
    scale = 1.0 / (2.0 * HALF_WIDTH)

    def ortho_blocks(item):
        fock_i, dens_i, ortho_i, fock_j, dens_j, ortho_j = item
        half_ii = product(fock_i, ortho_i).astype(low)
        half_jj = product(fock_j, ortho_j).astype(low)
        coupling = (0.5 * (product(fock_i, dens_j) + product(dens_i, fock_j))).astype(low)
        half_ij = product(coupling, ortho_j).astype(low)
        return turned(ortho_i, half_ii), turned(ortho_i, half_ij), turned(ortho_j, half_jj)

    def starts(blocks):
        o_ii, o_ij, o_jj = blocks
        s_ij = -o_ij * scale
        return (
            (middle - o_ii * scale).astype(low),
            s_ij.astype(low),
            s_ij.T.astype(low),
            (middle - o_jj * scale).astype(low),
        )

    def times(a, b):
        return (
            product(a[0], b[0]) + product(a[1], b[2]),
            product(a[0], b[1]) + product(a[1], b[3]),
            product(a[2], b[0]) + product(a[3], b[2]),
            product(a[2], b[1]) + product(a[3], b[3]),
        )

    def purified(q, c):
        return (3.0 * q.astype(jnp.float32) - 2.0 * c).astype(low).astype(jnp.float32)

    def energy(item, o, q, c):
        fock_i, dens_i, _, fock_j, dens_j, _ = item
        o_ii, o_ij, o_jj = o
        terms = purified(q[0], c[0]) * o_ii + purified(q[3], c[3]) * o_jj
        terms = terms + (purified(q[1], c[1]) + purified(q[2], c[2]).T) * o_ij
        terms = terms - dens_i.astype(jnp.float32) * fock_i.astype(jnp.float32)
        terms = terms - dens_j.astype(jnp.float32) * fock_j.astype(jnp.float32)
        return jnp.sum(terms)

    o = stage(ortho_blocks, operands)
    s = stage(starts, o)
    q = stage(lambda a: tuple(x.astype(low) for x in times(a, a)), s)
    c = stage(times, q, s)
    return stage(energy, operands, o, q, c)


def lists_kernel(choice_ref, slot_ref, place_ref, load0_ref, list_ref, load_ref):
    mine = place_ref[0]
    list_ref[2, 1] = mine & 7

    @pl.loop(0, load_ref.shape[0])
    def _(d):
        load_ref[d] = load0_ref[d]

    def step(k, filled):
        word = choice_ref[k]
        straight = word & 31
        crossed = lax.shift_right_logical(word, 5) & 31
        free = lax.shift_right_logical(word, 24)
        turn = (load_ref[crossed] < load_ref[straight]) & (free > 0)
        chosen = jnp.where(turn, crossed, straight)
        load_ref[chosen] = load_ref[chosen] + free
        list_ref[0, filled] = lax.shift_right_logical(word, jnp.where(turn, 17, 10)) & 127
        list_ref[1, filled] = slot_ref[k]
        return filled + (chosen == mine).astype(jnp.int32)

    list_ref[2, 0] = lax.fori_loop(0, choice_ref.shape[0], step, 0, unroll=4)


def dimer_lists(group_pairs, group_assign, owner_map, base, x, z, width, depth):
    count = group_pairs.shape[1]
    members = width * depth
    assert (width, depth) == (4, 8)
    fragments = jnp.arange(owner_map.shape[0], dtype=jnp.int32)
    rows = jnp.sum(
        jnp.where(group_pairs[:, :, None] == fragments, owner_map, 0), axis=2, dtype=jnp.int32
    ) - base
    first, second = rows[0], rows[1]
    foreign = (second >= members).astype(jnp.int32)
    second = second - members * foreign
    x_i, z_i = first >> 3, first & 7
    x_j, z_j = second >> 3, second & 7
    straight = x_i * 8 + z_j
    crossed = x_j * 8 + z_i
    near_i, near_j = (z - z_i) & 7, (z - z_j) & 7
    side_i, side_j = (x - x_i) & 3, (x - x_j) & 3
    straight_code = near_i | (8 + 4 * foreign + side_j) << 3
    crossed_code = side_i | near_j << 2
    choice = straight | crossed << 5 | straight_code << 10 | crossed_code << 17 | (1 - foreign) << 24
    order = jnp.arange(count, dtype=jnp.int32)
    same = group_assign[:, None] == group_assign[None, :]
    slot = jnp.sum((same & (order[None, :] < order[:, None])).astype(jnp.int32), axis=1)
    devices = jnp.arange(members, dtype=jnp.int32)
    load = jnp.sum(jnp.where(straight[None, :] == devices[:, None], foreign[None, :], 0), axis=1)
    smem = pl.BlockSpec(memory_space=pltpu.SMEM)
    return pl.pallas_call(
        lists_kernel,
        in_specs=[smem] * 4,
        out_specs=smem,
        out_shape=jax.ShapeDtypeStruct((3, count + LANES), jnp.int32),
        scratch_shapes=[pltpu.SMEM((members,), jnp.int32)],
        cost_estimate=pl.CostEstimate(flops=2 * 10**9, bytes_accessed=count * 32, transcendentals=0),
        name="dimer_lists",
    )(choice, group_assign << 5 | slot, (x * depth + z)[None], load)


def dimers_kernel(layout, list_ref, *refs):
    sources, (out_ref, fock_ref, dens_ref, ortho_ref, sems) = refs[:-5], refs[-5:]
    pools = (fock_ref, dens_ref, ortho_ref)
    members, lanes = out_ref.shape
    copies = [
        pltpu.make_async_copy(sources[source].at[index], pools[pool].at[entry], sems.at[pool, entry])
        for pool, entry, source, index in layout
    ]
    for copy in copies:
        copy.start()
    rows = lax.broadcasted_iota(jnp.int32, (members, lanes), 0)
    columns = lax.broadcasted_iota(jnp.int32, (members, lanes), 1)
    out_ref[...] = jnp.zeros_like(out_ref)
    for copy in copies:
        copy.wait()
    count = list_ref[2, 0]
    z = list_ref[2, 1]

    def at(entry):
        return jnp.where(entry < 8, (z - entry) & 7, entry)

    @pl.loop(0, (count + 1) >> 1)
    def _(pair):
        operands, heres = [], []
        for part in range(2):
            position = 2 * pair + part
            real = position < count
            position = jnp.where(real, position, 0)
            word, place = list_ref[0, position], list_ref[1, position]
            straight = word >= 64
            i = jnp.where(straight, word & 7, 8 + (word & 3))
            j = jnp.where(straight, lax.shift_right_logical(word, 3), lax.shift_right_logical(word, 2))
            operands.append(
                (fock_ref[at(i)], dens_ref[i], ortho_ref[at(i)], fock_ref[at(j)], dens_ref[j], ortho_ref[at(j)])
            )
            target, slot = lax.shift_right_logical(place, 5), place & 31
            here = ((rows == target) & (columns == slot)) | (columns == lanes - 1)
            heres.append(here & real)
        energies = dimer_terms(operands)
        update = out_ref[...]
        for here, energy in zip(heres, energies):
            update = update + jnp.where(here, energy, 0.0)
        out_ref[...] = update


def dimer_energies(lists, fock, dens, ortho, members):
    arrays, layout = [], []
    for pool, entries in enumerate((fock, dens, ortho)):
        for entry, (array, index) in enumerate(entries):
            where = next((k for k, a in enumerate(arrays) if a is array), len(arrays))
            if where == len(arrays):
                arrays.append(array)
            layout.append((pool, entry, where, index))
    size = arrays[0].shape[1]
    flops = 14 * 26 * 2 * size**3
    vmem = pl.BlockSpec(memory_space=pltpu.VMEM)
    return pl.pallas_call(
        functools.partial(dimers_kernel, layout),
        in_specs=[pl.BlockSpec(memory_space=pltpu.SMEM)]
        + [pl.BlockSpec(memory_space=pltpu.HBM)] * len(arrays),
        out_specs=vmem,
        out_shape=jax.ShapeDtypeStruct((members, LANES), jnp.float32),
        scratch_shapes=[pltpu.VMEM((16, size, size), jnp.bfloat16)] * 3
        + [pltpu.SemaphoreType.DMA((3, 16))],
        compiler_params=pltpu.CompilerParams(vmem_limit_bytes=62 * 1024 * 1024),
        cost_estimate=pl.CostEstimate(flops=flops, bytes_accessed=16 * 6 * size**2, transcendentals=0),
        name="dimer_energies",
    )(lists, *arrays)


def on_device(
    densities,
    core_hamiltonian,
    embedding,
    fit_factors,
    orthogonalizers,
    pairs,
    assignment,
    owner_map,
):
    width, depth = lax.axis_size("dev_0"), lax.axis_size("dev_1")
    members = width * depth
    group_index = lax.axis_index("grp")

    dens_column = along_line(densities, "dev_0")
    pieces = along_ring(jnp.concatenate(dens_column), "dev_1")
    half = depth // 2
    early = jnp.concatenate(pieces[half + 1 :] + pieces[:half])
    coeffs = [coefficients(rows, fit_factors) for rows in (pieces[half], early)]
    coeffs = jnp.concatenate(coeffs).reshape(depth, width, -1)
    row_index = lax.axis_index("dev_1")
    coeffs = jnp.concatenate([coeffs[::-1], coeffs[::-1]])
    first = (half - 1 - row_index + depth) % depth
    coeffs = lax.dynamic_slice_in_dim(coeffs, first, depth, 0)
    coeffs = coeffs.swapaxes(0, 1).reshape(members, -1).astype(jnp.bfloat16)
    terms = jnp.einsum(
        "rp,pmn->rmn", coeffs, fit_factors, preferred_element_type=jnp.float32
    ).astype(jnp.bfloat16)
    chunks = [terms[k * depth : (k + 1) * depth] for k in range(width)]
    column_sum = summed_columns(chunks, "dev_0")
    coulomb = exchanged(column_sum, "dev_1").astype(jnp.float32).sum(axis=0, keepdims=True)
    fock = (
        core_hamiltonian.astype(jnp.float32) + embedding.astype(jnp.float32) + coulomb
    ).astype(jnp.bfloat16)

    ortho_row = exchanged(jnp.concatenate([orthogonalizers] * depth), "dev_1")
    ortho_column = along_line(orthogonalizers, "dev_0")
    next_dens = from_behind(jnp.concatenate(dens_column), "grp", -1)
    next_ortho = from_behind(jnp.concatenate(ortho_column), "grp", -1)
    fock_column = along_line(fock, "dev_0")
    fock_row = exchanged(jnp.concatenate([fock] * depth), "dev_1")
    next_fock = from_behind(jnp.concatenate(fock_column), "grp", -1)

    dim_group = pairs.shape[0] // lax.axis_size("grp")
    start = group_index * dim_group
    group_pairs = lax.dynamic_slice_in_dim(pairs.T, start, dim_group, 1)
    group_assign = lax.dynamic_slice_in_dim(assignment, start, dim_group, 0)
    lists = dimer_lists(
        group_pairs,
        group_assign,
        owner_map,
        (group_index * members).astype(jnp.int32),
        lax.axis_index("dev_0").astype(jnp.int32),
        lax.axis_index("dev_1").astype(jnp.int32),
        width,
        depth,
    )

    def whole(arrays):
        return [(a, 0) for a in arrays]

    def parts(array):
        return [(array, k) for k in range(array.shape[0])]

    sent = dimer_energies(
        lists,
        parts(fock_row) + whole(fock_column) + parts(next_fock),
        whole(pieces + dens_column) + parts(next_dens),
        parts(ortho_row) + whole(ortho_column) + parts(next_ortho),
        members,
    )
    arrived = lax.all_to_all(
        sent.reshape(members, 1, LANES), DEV, split_axis=0, concat_axis=0, tiled=True
    )
    mine = jnp.sum(arrived, axis=(0, 1))
    group_sums = sent_to_all(mine[LANES - 1 :], "grp")
    return (mine[:SLOTS], jnp.sum(group_sums))


def solution(mesh):
    torus = Mesh(mesh.devices.reshape(mesh.shape["grp"], 4, 8), ("grp", "dev_0", "dev_1"))
    in_specs = (
        P(GRP_DEV, None, None),
        P(GRP_DEV, None, None),
        P(GRP_DEV, None, None),
        P(DEV, None, None),
        P(GRP_DEV, None, None),
        P(),
        P(),
        P(),
    )
    out_specs = (P(GRP_DEV), P())

    return jax.shard_map(on_device, mesh=torus, in_specs=in_specs, out_specs=out_specs, check_vma=False)
```

profile of v0, /device:TPU:1, one launch (start us, length us, event | category | flops | bytes accessed | tf_op | source)
XLA Modules:
  0.0 207.4 jit_solution(17909167383376465312)
XLA Ops:
  0.7 2.1 %collective-permute-start = (bf16[1,200,200]{2,1,0:T(8,128)(2,1)}, bf16[1,200,200]{2,1,0:T(8,128)(2,1)S(1)}, u32[]{:S(2)}, u32[]{:S(2)}) collective-permute-start(bf16[1,200,200]{2,1,0:T(8,128)(2,1)} %refs_14_.1), channel_id=1, source_target_pairs={{0,8},{8,16},{16,24},{24,0},{1,9},{9,17},{17,25},{25,1},{2,10},{10... | collective-permute-start | bytes 240008 | tf_op jit(solution)/shard_map/ppermute | solution.py:20
  2.8 2.5 %collective-permute-start.1 = (bf16[1,200,200]{2,1,0:T(8,128)(2,1)}, bf16[1,200,200]{2,1,0:T(8,128)(2,1)S(1)}, u32[]{:S(2)}, u32[]{:S(2)}) collective-permute-start(bf16[1,200,200]{2,1,0:T(8,128)(2,1)} %refs_14_.1), channel_id=1, source_target_pairs={{0,16},{8,24},{16,0},{24,8},{1,17},{9,25},{17,1},{25,9},{2,18},{10... | collective-permute-start | bytes 240008 | tf_op jit(solution)/shard_map/ppermute | solution.py:20
  11.0 5.6 %collective-permute-start.7 = (bf16[4,200,200]{2,1,0:T(8,128)(2,1)}, bf16[4,200,200]{2,1,0:T(8,128)(2,1)S(1)}, u32[]{:S(2)}, u32[]{:S(2)}) collective-permute-start(bf16[4,200,200]{2,1,0:T(8,128)(2,1)} %constant_dynamic-update-slice_fusion.refs_6_), channel_id=1, source_target_pairs={{0,7},{1,0},{2,1},{3,2},{4,3},{5,4},{6,5},{7,6},{8,15},{9,8},{10,9... | collective-permute-start | bytes 960008 | tf_op jit(solution)/shard_map/ppermute | solution.py:20
  16.6 7.3 %collective-permute-done.7.refs_13_ = bf16[4,200,200]{2,1,0:T(8,128)(2,1)S(1)} collective-permute-done((bf16[4,200,200]{2,1,0:T(8,128)(2,1)}, bf16[4,200,200]{2,1,0:T(8,128)(2,1)S(1)}, u32[]{:S(2)}, u32[]{:S(2)}) %collective-permute-start.7) | collective-permute-done | bytes 320032 | tf_op jit(solution)/shard_map/ppermute | solution.py:20
  23.9 3.3 %collective-permute-start.8 = (bf16[4,200,200]{2,1,0:T(8,128)(2,1)S(1)}, bf16[4,200,200]{2,1,0:T(8,128)(2,1)S(1)}, u32[]{:S(2)}, u32[]{:S(2)}) collective-permute-start(bf16[4,200,200]{2,1,0:T(8,128)(2,1)S(1)} %collective-permute-done.7.refs_13_), channel_id=1, source_target_pairs={{0,7},{1,0},{2,1},{3,2},{4,3},{5,4},{6,5},{7,6},{8,15},{9,8},{10,9... | collective-permute-start | bytes 960008 | tf_op jit(solution)/shard_map/ppermute | solution.py:20
  27.2 6.1 %collective-permute-done.8.refs_12_ = bf16[4,200,200]{2,1,0:T(8,128)(2,1)S(1)} collective-permute-done((bf16[4,200,200]{2,1,0:T(8,128)(2,1)S(1)}, bf16[4,200,200]{2,1,0:T(8,128)(2,1)S(1)}, u32[]{:S(2)}, u32[]{:S(2)}) %collective-permute-start.8) | collective-permute-done | bytes 320032 | tf_op jit(solution)/shard_map/ppermute | solution.py:20
  33.4 3.4 %collective-permute-start.9 = (bf16[4,200,200]{2,1,0:T(8,128)(2,1)S(1)}, bf16[4,200,200]{2,1,0:T(8,128)(2,1)S(1)}, u32[]{:S(2)}, u32[]{:S(2)}) collective-permute-start(bf16[4,200,200]{2,1,0:T(8,128)(2,1)S(1)} %collective-permute-done.8.refs_12_), channel_id=1, source_target_pairs={{0,7},{1,0},{2,1},{3,2},{4,3},{5,4},{6,5},{7,6},{8,15},{9,8},{10,9... | collective-permute-start | bytes 960008 | tf_op jit(solution)/shard_map/ppermute | solution.py:20
  36.9 5.2 %collective-permute-done.9.refs_11_ = bf16[4,200,200]{2,1,0:T(8,128)(2,1)S(1)} collective-permute-done((bf16[4,200,200]{2,1,0:T(8,128)(2,1)S(1)}, bf16[4,200,200]{2,1,0:T(8,128)(2,1)S(1)}, u32[]{:S(2)}, u32[]{:S(2)}) %collective-permute-start.9) | collective-permute-done | bytes 320032 | tf_op jit(solution)/shard_map/ppermute | solution.py:20
  43.4 2.1 %collective-permute-done.5.refs_9_ = bf16[4,200,200]{2,1,0:T(8,128)(2,1)S(1)} collective-permute-done((bf16[4,200,200]{2,1,0:T(8,128)(2,1)}, bf16[4,200,200]{2,1,0:T(8,128)(2,1)S(1)}, u32[]{:S(2)}, u32[]{:S(2)}) %collective-permute-start.5) | collective-permute-done | bytes 320032 | tf_op jit(solution)/shard_map/ppermute | solution.py:20
  45.6 2.7 %collective-permute-start.10 = (bf16[2,200,200]{2,1,0:T(8,128)(2,1)S(1)}, bf16[2,200,200]{2,1,0:T(8,128)(2,1)S(1)}, u32[]{:S(2)}, u32[]{:S(2)}) collective-permute-start(bf16[2,200,200]{2,1,0:T(8,128)(2,1)S(1)} %slice.74), channel_id=1, source_target_pairs={{0,7},{1,0},{2,1},{3,2},{4,3},{5,4},{6,5},{7,6},{8,15},{9,8},{10,9... | collective-permute-start | bytes 480008 | tf_op jit(solution)/shard_map/ppermute | solution.py:20
  54.3 3.0 %collective-permute-start.12 = (bf16[8,104,200]{2,0,1:T(8,128)(2,1)S(1)}, bf16[8,104,200]{2,0,1:T(8,128)(2,1)S(1)}, u32[]{:S(2)}, u32[]{:S(2)}) collective-permute-start(bf16[8,104,200]{2,0,1:T(8,128)(2,1)S(1)} %get-tuple-element.9), channel_id=1, source_target_pairs={{0,24},{8,0},{16,8},{24,16},{1,25},{9,1},{17,9},{25,17},{2,26},{10... | collective-permute-start | bytes 998408 | tf_op jit(solution)/shard_map/ppermute | solution.py:20
  57.3 2.7 %collective-permute-start.16 = (bf16[8,96,200]{2,0,1:T(8,128)(2,1)S(1)}, bf16[8,96,200]{2,0,1:T(8,128)(2,1)S(1)}, u32[]{:S(2)}, u32[]{:S(2)}) collective-permute-start(bf16[8,96,200]{2,0,1:T(8,128)(2,1)S(1)} %get-tuple-element.11), channel_id=1, source_target_pairs={{0,24},{8,0},{16,8},{24,16},{1,25},{9,1},{17,9},{25,17},{2,26},{10... | collective-permute-start | bytes 921608 | tf_op jit(solution)/shard_map/ppermute | solution.py:20
  60.0 2.3 %collective-permute-done.14 = bf16[8,96,200]{2,0,1:T(8,128)(2,1)S(1)} collective-permute-done((bf16[8,96,200]{2,0,1:T(8,128)(2,1)S(1)}, bf16[8,96,200]{2,0,1:T(8,128)(2,1)S(1)}, u32[]{:S(2)}, u32[]{:S(2)}) %collective-permute-start.14) | collective-permute-done | bytes 307232 | tf_op jit(solution)/shard_map/ppermute | solution.py:20
  62.7 3.0 %collective-permute-start.13 = (bf16[8,104,200]{2,0,1:T(8,128)(2,1)S(1)}, bf16[8,104,200]{2,0,1:T(8,128)(2,1)S(1)}, u32[]{:S(2)}, u32[]{:S(2)}) collective-permute-start(bf16[8,104,200]{2,0,1:T(8,128)(2,1)S(1)} %add_convert_fusion.1), channel_id=1, source_target_pairs={{0,24},{8,0},{16,8},{24,16},{1,25},{9,1},{17,9},{25,17},{2,26},{10... | collective-permute-start | bytes 998408 | tf_op jit(solution)/shard_map/ppermute | solution.py:20
  65.7 3.4 %collective-permute-done.16 = bf16[8,96,200]{2,0,1:T(8,128)(2,1)S(1)} collective-permute-done((bf16[8,96,200]{2,0,1:T(8,128)(2,1)S(1)}, bf16[8,96,200]{2,0,1:T(8,128)(2,1)S(1)}, u32[]{:S(2)}, u32[]{:S(2)}) %collective-permute-start.16) | collective-permute-done | bytes 307232 | tf_op jit(solution)/shard_map/ppermute | solution.py:20
  69.1 9.3 %collective-permute-done.15 = bf16[8,96,200]{2,0,1:T(8,128)(2,1)S(1)} collective-permute-done((bf16[8,96,200]{2,0,1:T(8,128)(2,1)S(1)}, bf16[8,96,200]{2,0,1:T(8,128)(2,1)S(1)}, u32[]{:S(2)}, u32[]{:S(2)}) %collective-permute-start.15) | collective-permute-done | bytes 307232 | tf_op jit(solution)/shard_map/ppermute | solution.py:20
  79.1 20.0 %all_to_all.26 = bf16[8,200,200]{2,1,0:T(8,128)(2,1)S(1)} all-to-all(bf16[8,200,200]{2,1,0:T(8,128)(2,1)S(1)} %copy.57), channel_id=1, replica_groups=mesh['grp'=8,'dev_0'=4,'dev_1'=8] {'dev_1'}, dimensions={0} | all-to-all | bytes 1280000 | tf_op jit(solution)/shard_map/all_to_all | solution.py:67
  100.0 3.7 %all-to-all-start.2 = ((bf16[8,200,200]{2,1,0:T(8,128)(2,1)}), bf16[8,200,200]{2,1,0:T(8,128)(2,1)S(1)}, u32[]{:S(2)}, u32[]{:S(2)}) async-start(bf16[8,200,200]{2,1,0:T(8,128)(2,1)} %concatenate.40), calls=%async_computation.2 | async-start | bytes 1638400 | tf_op jit(solution)/shard_map/all_to_all | solution.py:67
  103.7 1.7 collective-permute-start.22
  105.4 2.2 %collective-permute-start.23 = (bf16[1,200,200]{2,1,0:T(8,128)(2,1)S(1)}, bf16[1,200,200]{2,1,0:T(8,128)(2,1)S(1)}, u32[]{:S(2)}, u32[]{:S(2)}) collective-permute-start(bf16[1,200,200]{2,1,0:T(8,128)(2,1)S(1)} %copy-done.7), channel_id=1, source_target_pairs={{0,16},{8,24},{16,0},{24,8},{1,17},{9,25},{17,1},{25,9},{2,18},{10... | collective-permute-start | bytes 240008 | tf_op jit(solution)/shard_map/ppermute | solution.py:20
  110.1 8.8 %all-to-all-done.2.refs_19_ = bf16[8,200,200]{2,1,0:T(8,128)(2,1)S(1)} async-done(((bf16[8,200,200]{2,1,0:T(8,128)(2,1)}), bf16[8,200,200]{2,1,0:T(8,128)(2,1)S(1)}, u32[]{:S(2)}, u32[]{:S(2)}) %all-to-all-start.2) | async-done | bytes 640032 | tf_op jit(solution)/shard_map/all_to_all | solution.py:67
  120.0 3.5 %all-to-all-start.1 = ((bf16[8,200,200]{2,1,0:T(8,128)(2,1)}), bf16[8,200,200]{2,1,0:T(8,128)(2,1)S(1)}, u32[]{:S(2)}, u32[]{:S(2)}) async-start(bf16[8,200,200]{2,1,0:T(8,128)(2,1)} %concatenate.38), calls=%async_computation.1 | async-start | bytes 1638400 | tf_op jit(solution)/shard_map/all_to_all | solution.py:67
  123.9 11.8 %collective-permute-start.21 = (bf16[4,200,200]{2,1,0:T(8,128)(2,1)}, bf16[4,200,200]{2,1,0:T(8,128)(2,1)}, u32[]{:S(2)}, u32[]{:S(2)}) collective-permute-start(bf16[4,200,200]{2,1,0:T(8,128)(2,1)} %constant_dynamic-update-slice_fusion.refs_6_), channel_id=1, source_target_pairs={{32,0},{64,32},{96,64},{128,96},{160,128},{192,160},{224,192},{33,... | collective-permute-start | bytes 960008 | tf_op jit(solution)/shard_map/ppermute | solution.py:26
  135.6 1.7 collective-permute-start.17
  137.3 2.4 %collective-permute-start.18 = (bf16[1,200,200]{2,1,0:T(8,128)(2,1)S(1)}, bf16[1,200,200]{2,1,0:T(8,128)(2,1)S(1)}, u32[]{:S(2)}, u32[]{:S(2)}) collective-permute-start(bf16[1,200,200]{2,1,0:T(8,128)(2,1)S(1)} %fusion.16.refs_1_), channel_id=1, source_target_pairs={{0,16},{8,24},{16,0},{24,8},{1,17},{9,25},{17,1},{25,9},{2,18},{10... | collective-permute-start | bytes 240008 | tf_op jit(solution)/shard_map/ppermute | solution.py:20
  141.0 2.1 %collective-permute-start.25 = (bf16[4,200,200]{2,1,0:T(8,128)(2,1)S(1)}, bf16[4,200,200]{2,1,0:T(8,128)(2,1)}, u32[]{:S(2)}, u32[]{:S(2)}) collective-permute-start(bf16[4,200,200]{2,1,0:T(8,128)(2,1)S(1)} %pad_maximum_fusion.2), channel_id=1, source_target_pairs={{32,0},{64,32},{96,64},{128,96},{160,128},{192,160},{224,192},{33,... | collective-permute-start | bytes 960008 | tf_op jit(solution)/shard_map/ppermute | solution.py:26
  143.1 1.9 collective-permute-done.18.refs_3_
  145.1 2.3 %collective-permute-start.20 = (bf16[4,200,200]{2,1,0:T(8,128)(2,1)S(1)}, bf16[4,200,200]{2,1,0:T(8,128)(2,1)}, u32[]{:S(2)}, u32[]{:S(2)}) collective-permute-start(bf16[4,200,200]{2,1,0:T(8,128)(2,1)S(1)} %pad_maximum_fusion.1), channel_id=1, source_target_pairs={{32,0},{64,32},{96,64},{128,96},{160,128},{192,160},{224,192},{33,... | collective-permute-start | bytes 960008 | tf_op jit(solution)/shard_map/ppermute | solution.py:26
  149.4 6.1 %dimer_lists.1.list_ref = s32[3,512]{1,0:T(4,128)} custom-call(s32[384]{0:T(512)} %get-tuple-element.13.choice_ref, s32[384]{0:T(512)} %get-tuple-element.12.slot_ref, s32[1]{0:T(128)} %bitcast.1.place_ref, s32[32]{0:T(128)} %select_reduce_fusion.1.load0_ref), custom_call_target="tpu_custom_call" | custom-call | flops 2000000000 | bytes 12288 | tf_op jit(solution)/shard_map/dimer_lists/pallas_call | solution.py:191
  156.6 20.4 %dimer_energies.1 = f32[32,128]{1,0:T(8,128)} custom-call(s32[3,512]{1,0:T(4,128)} %dimer_lists.1.list_ref, bf16[8,200,200]{2,1,0:T(8,128)(2,1)} %copy-done.6, bf16[1,200,200]{2,1,0:T(8,128)(2,1)} %copy-done.2, bf16[1,200,200]{2,1,0:T(8,128)(2,1)} %copy-done.21, bf16[1,200,200]{2,1,0:T(8,128)(2,1)} %copy-done.22, bf16[1,200,200]{2,1,0:T(8,128)(2,1)} %copy-done.23, ...), custom_call_target="tpu_custom_call" | custom-call | flops 5824000000 | bytes 3840000 | tf_op jit(solution)/shard_map/dimer_energies/pallas_call | solution.py:258
  177.0 16.8 %all_to_all.27 = f32[32,1,128]{2,1,0:T(1,128)S(1)} all-to-all(f32[32,1,128]{2,1,0:T(1,128)} %bitcast.29), channel_id=1, replica_groups=mesh['grp'=8,'dev_0'=4,'dev_1'=8] {'dev_0','dev_1'}, dimensions={0} | all-to-all | bytes 32768 | tf_op jit(solution)/shard_map/all_to_all | solution.py:343
  195.1 11.7 %all_to_all.28 = f32[8,1,1]{2,1,0:T(1,128)S(1)} all-to-all(f32[8,1,1]{2,1,0:T(1,128)S(1)} %broadcast_in_dim.51), channel_id=1, replica_groups=mesh['grp'=8,'dev_0'=4,'dev_1'=8] {'grp'}, dimensions={0} | all-to-all | bytes 64 | tf_op jit(solution)/shard_map/all_to_all | solution.py:72
  (138 shorter events, 25.1 us)
Async XLA Ops:
  0.6 109.0 %copy-start = (s32[3072,2]{0,1:T(2,128)S(1)}, s32[3072,2]{0,1:T(2,128)}, u32[]{:S(2)}) copy-start(s32[3072,2]{0,1:T(2,128)} %param.13) | copy-start | bytes 73732
  0.6 42.7 %copy-start.12 = (bf16[1,200,200]{2,1,0:T(8,128)(2,1)S(1)}, bf16[1,200,200]{2,1,0:T(8,128)(2,1)}, u32[]{:S(2)}) copy-start(bf16[1,200,200]{2,1,0:T(8,128)(2,1)} %refs_14_.1) | copy-start | bytes 240004
  0.7 7.3 %collective-permute-start = (bf16[1,200,200]{2,1,0:T(8,128)(2,1)}, bf16[1,200,200]{2,1,0:T(8,128)(2,1)S(1)}, u32[]{:S(2)}, u32[]{:S(2)}) collective-permute-start(bf16[1,200,200]{2,1,0:T(8,128)(2,1)} %refs_14_.1), channel_id=1, source_target_pairs={{0,8},{8,16},{16,24},{24,0},{1,9},{9,17},{17,25},{25,1},{2,10},{10... | collective-permute-start | bytes 240008 | tf_op jit(solution)/shard_map/ppermute | solution.py:20
  2.8 6.9 %collective-permute-start.1 = (bf16[1,200,200]{2,1,0:T(8,128)(2,1)}, bf16[1,200,200]{2,1,0:T(8,128)(2,1)S(1)}, u32[]{:S(2)}, u32[]{:S(2)}) collective-permute-start(bf16[1,200,200]{2,1,0:T(8,128)(2,1)} %refs_14_.1), channel_id=1, source_target_pairs={{0,16},{8,24},{16,0},{24,8},{1,17},{9,25},{17,1},{25,9},{2,18},{10... | collective-permute-start | bytes 240008 | tf_op jit(solution)/shard_map/ppermute | solution.py:20
  5.2 5.1 %collective-permute-start.2 = (bf16[1,200,200]{2,1,0:T(8,128)(2,1)}, bf16[1,200,200]{2,1,0:T(8,128)(2,1)S(1)}, u32[]{:S(2)}, u32[]{:S(2)}) collective-permute-start(bf16[1,200,200]{2,1,0:T(8,128)(2,1)} %refs_14_.1), channel_id=1, source_target_pairs={{0,24},{8,0},{16,8},{24,16},{1,25},{9,1},{17,9},{25,17},{2,26},{10... | collective-permute-start | bytes 240008 | tf_op jit(solution)/shard_map/ppermute | solution.py:20
  7.9 41.6 %copy-start.13 = (bf16[1,200,200]{2,1,0:T(8,128)(2,1)}, bf16[1,200,200]{2,1,0:T(8,128)(2,1)S(1)}, u32[]{:S(2)}) copy-start(bf16[1,200,200]{2,1,0:T(8,128)(2,1)S(1)} %collective-permute-done.refs_15_) | copy-start | bytes 240004
  11.0 12.9 %collective-permute-start.7 = (bf16[4,200,200]{2,1,0:T(8,128)(2,1)}, bf16[4,200,200]{2,1,0:T(8,128)(2,1)S(1)}, u32[]{:S(2)}, u32[]{:S(2)}) collective-permute-start(bf16[4,200,200]{2,1,0:T(8,128)(2,1)} %constant_dynamic-update-slice_fusion.refs_6_), channel_id=1, source_target_pairs={{0,7},{1,0},{2,1},{3,2},{4,3},{5,4},{6,5},{7,6},{8,15},{9,8},{10,9... | collective-permute-start | bytes 960008 | tf_op jit(solution)/shard_map/ppermute | solution.py:20
  16.6 10.6 %collective-permute-start.3 = (bf16[4,200,200]{2,1,0:T(8,128)(2,1)}, bf16[4,200,200]{2,1,0:T(8,128)(2,1)S(1)}, u32[]{:S(2)}, u32[]{:S(2)}) collective-permute-start(bf16[4,200,200]{2,1,0:T(8,128)(2,1)} %constant_dynamic-update-slice_fusion.refs_6_), channel_id=1, source_target_pairs={{0,1},{1,2},{2,3},{3,4},{4,5},{5,6},{6,7},{7,0},{8,9},{9,10},{10,1... | collective-permute-start | bytes 960008 | tf_op jit(solution)/shard_map/ppermute | solution.py:20
  23.9 9.4 %collective-permute-start.8 = (bf16[4,200,200]{2,1,0:T(8,128)(2,1)S(1)}, bf16[4,200,200]{2,1,0:T(8,128)(2,1)S(1)}, u32[]{:S(2)}, u32[]{:S(2)}) collective-permute-start(bf16[4,200,200]{2,1,0:T(8,128)(2,1)S(1)} %collective-permute-done.7.refs_13_), channel_id=1, source_target_pairs={{0,7},{1,0},{2,1},{3,2},{4,3},{5,4},{6,5},{7,6},{8,15},{9,8},{10,9... | collective-permute-start | bytes 960008 | tf_op jit(solution)/shard_map/ppermute | solution.py:20
  27.2 9.6 %collective-permute-start.4 = (bf16[4,200,200]{2,1,0:T(8,128)(2,1)S(1)}, bf16[4,200,200]{2,1,0:T(8,128)(2,1)}, u32[]{:S(2)}, u32[]{:S(2)}) collective-permute-start(bf16[4,200,200]{2,1,0:T(8,128)(2,1)S(1)} %collective-permute-done.3.refs_7_), channel_id=1, source_target_pairs={{0,1},{1,2},{2,3},{3,4},{4,5},{5,6},{6,7},{7,0},{8,9},{9,10},{10,1... | collective-permute-start | bytes 960008 | tf_op jit(solution)/shard_map/ppermute | solution.py:20
  33.4 8.7 %collective-permute-start.9 = (bf16[4,200,200]{2,1,0:T(8,128)(2,1)S(1)}, bf16[4,200,200]{2,1,0:T(8,128)(2,1)S(1)}, u32[]{:S(2)}, u32[]{:S(2)}) collective-permute-start(bf16[4,200,200]{2,1,0:T(8,128)(2,1)S(1)} %collective-permute-done.8.refs_12_), channel_id=1, source_target_pairs={{0,7},{1,0},{2,1},{3,2},{4,3},{5,4},{6,5},{7,6},{8,15},{9,8},{10,9... | collective-permute-start | bytes 960008 | tf_op jit(solution)/shard_map/ppermute | solution.py:20
  36.8 8.7 %collective-permute-start.5 = (bf16[4,200,200]{2,1,0:T(8,128)(2,1)}, bf16[4,200,200]{2,1,0:T(8,128)(2,1)S(1)}, u32[]{:S(2)}, u32[]{:S(2)}) collective-permute-start(bf16[4,200,200]{2,1,0:T(8,128)(2,1)} %collective-permute-done.4.refs_8_), channel_id=1, source_target_pairs={{0,1},{1,2},{2,3},{3,4},{4,5},{5,6},{6,7},{7,0},{8,9},{9,10},{10,1... | collective-permute-start | bytes 960008 | tf_op jit(solution)/shard_map/ppermute | solution.py:20
  45.5 6.2 %collective-permute-start.6 = (bf16[2,200,200]{2,1,0:T(8,128)(2,1)S(1)}, bf16[2,200,200]{2,1,0:T(8,128)(2,1)S(1)}, u32[]{:S(2)}, u32[]{:S(2)}) collective-permute-start(bf16[2,200,200]{2,1,0:T(8,128)(2,1)S(1)} %slice.73), channel_id=1, source_target_pairs={{0,1},{1,2},{2,3},{3,4},{4,5},{5,6},{6,7},{7,0},{8,9},{9,10},{10,1... | collective-permute-start | bytes 480008 | tf_op jit(solution)/shard_map/ppermute | solution.py:20
  45.6 6.1 %collective-permute-start.10 = (bf16[2,200,200]{2,1,0:T(8,128)(2,1)S(1)}, bf16[2,200,200]{2,1,0:T(8,128)(2,1)S(1)}, u32[]{:S(2)}, u32[]{:S(2)}) collective-permute-start(bf16[2,200,200]{2,1,0:T(8,128)(2,1)S(1)} %slice.74), channel_id=1, source_target_pairs={{0,7},{1,0},{2,1},{3,2},{4,3},{5,4},{6,5},{7,6},{8,15},{9,8},{10,9... | collective-permute-start | bytes 480008 | tf_op jit(solution)/shard_map/ppermute | solution.py:20
  53.9 8.4 %collective-permute-start.14 = (bf16[8,96,200]{2,0,1:T(8,128)(2,1)S(1)}, bf16[8,96,200]{2,0,1:T(8,128)(2,1)S(1)}, u32[]{:S(2)}, u32[]{:S(2)}) collective-permute-start(bf16[8,96,200]{2,0,1:T(8,128)(2,1)S(1)} %get-tuple-element.10), channel_id=1, source_target_pairs={{0,8},{8,16},{16,24},{24,0},{1,9},{9,17},{17,25},{25,1},{2,10},{10... | collective-permute-start | bytes 921608 | tf_op jit(solution)/shard_map/ppermute | solution.py:20
  54.3 8.3 %collective-permute-start.12 = (bf16[8,104,200]{2,0,1:T(8,128)(2,1)S(1)}, bf16[8,104,200]{2,0,1:T(8,128)(2,1)S(1)}, u32[]{:S(2)}, u32[]{:S(2)}) collective-permute-start(bf16[8,104,200]{2,0,1:T(8,128)(2,1)S(1)} %get-tuple-element.9), channel_id=1, source_target_pairs={{0,24},{8,0},{16,8},{24,16},{1,25},{9,1},{17,9},{25,17},{2,26},{10... | collective-permute-start | bytes 998408 | tf_op jit(solution)/shard_map/ppermute | solution.py:20
  57.3 21.2 %collective-permute-start.11 = (bf16[8,104,200]{2,0,1:T(8,128)(2,1)S(1)}, bf16[8,104,200]{2,0,1:T(8,128)(2,1)S(1)}, u32[]{:S(2)}, u32[]{:S(2)}) collective-permute-start(bf16[8,104,200]{2,0,1:T(8,128)(2,1)S(1)} %get-tuple-element.8), channel_id=1, source_target_pairs={{0,8},{8,16},{16,24},{24,0},{1,9},{9,17},{17,25},{25,1},{2,10},{10... | collective-permute-start | bytes 998408 | tf_op jit(solution)/shard_map/ppermute | solution.py:20
  57.3 11.8 %collective-permute-start.16 = (bf16[8,96,200]{2,0,1:T(8,128)(2,1)S(1)}, bf16[8,96,200]{2,0,1:T(8,128)(2,1)S(1)}, u32[]{:S(2)}, u32[]{:S(2)}) collective-permute-start(bf16[8,96,200]{2,0,1:T(8,128)(2,1)S(1)} %get-tuple-element.11), channel_id=1, source_target_pairs={{0,24},{8,0},{16,8},{24,16},{1,25},{9,1},{17,9},{25,17},{2,26},{10... | collective-permute-start | bytes 921608 | tf_op jit(solution)/shard_map/ppermute | solution.py:20
  62.5 15.9 %collective-permute-start.15 = (bf16[8,96,200]{2,0,1:T(8,128)(2,1)S(1)}, bf16[8,96,200]{2,0,1:T(8,128)(2,1)S(1)}, u32[]{:S(2)}, u32[]{:S(2)}) collective-permute-start(bf16[8,96,200]{2,0,1:T(8,128)(2,1)S(1)} %add_convert_fusion.3), channel_id=1, source_target_pairs={{0,8},{8,16},{16,24},{24,0},{1,9},{9,17},{17,25},{25,1},{2,10},{10... | collective-permute-start | bytes 921608 | tf_op jit(solution)/shard_map/ppermute | solution.py:20
  62.7 15.8 %collective-permute-start.13 = (bf16[8,104,200]{2,0,1:T(8,128)(2,1)S(1)}, bf16[8,104,200]{2,0,1:T(8,128)(2,1)S(1)}, u32[]{:S(2)}, u32[]{:S(2)}) collective-permute-start(bf16[8,104,200]{2,0,1:T(8,128)(2,1)S(1)} %add_convert_fusion.1), channel_id=1, source_target_pairs={{0,24},{8,0},{16,8},{24,16},{1,25},{9,1},{17,9},{25,17},{2,26},{10... | collective-permute-start | bytes 998408 | tf_op jit(solution)/shard_map/ppermute | solution.py:20
  100.0 18.9 %all-to-all-start.2 = ((bf16[8,200,200]{2,1,0:T(8,128)(2,1)}), bf16[8,200,200]{2,1,0:T(8,128)(2,1)S(1)}, u32[]{:S(2)}, u32[]{:S(2)}) async-start(bf16[8,200,200]{2,1,0:T(8,128)(2,1)} %concatenate.40), calls=%async_computation.2 | async-start | bytes 1638400 | tf_op jit(solution)/shard_map/all_to_all | solution.py:67
  103.7 33.6 %collective-permute-start.22 = (bf16[1,200,200]{2,1,0:T(8,128)(2,1)S(1)}, bf16[1,200,200]{2,1,0:T(8,128)(2,1)S(1)}, u32[]{:S(2)}, u32[]{:S(2)}) collective-permute-start(bf16[1,200,200]{2,1,0:T(8,128)(2,1)S(1)} %copy-done.7), channel_id=1, source_target_pairs={{0,8},{8,16},{16,24},{24,0},{1,9},{9,17},{17,25},{25,1},{2,10},{10... | collective-permute-start | bytes 240008 | tf_op jit(solution)/shard_map/ppermute | solution.py:20
  105.4 34.3 %collective-permute-start.23 = (bf16[1,200,200]{2,1,0:T(8,128)(2,1)S(1)}, bf16[1,200,200]{2,1,0:T(8,128)(2,1)S(1)}, u32[]{:S(2)}, u32[]{:S(2)}) collective-permute-start(bf16[1,200,200]{2,1,0:T(8,128)(2,1)S(1)} %copy-done.7), channel_id=1, source_target_pairs={{0,16},{8,24},{16,0},{24,8},{1,17},{9,25},{17,1},{25,9},{2,18},{10... | collective-permute-start | bytes 240008 | tf_op jit(solution)/shard_map/ppermute | solution.py:20
  107.6 33.3 %collective-permute-start.24 = (bf16[1,200,200]{2,1,0:T(8,128)(2,1)S(1)}, bf16[1,200,200]{2,1,0:T(8,128)(2,1)S(1)}, u32[]{:S(2)}, u32[]{:S(2)}) collective-permute-start(bf16[1,200,200]{2,1,0:T(8,128)(2,1)S(1)} %copy-done.7), channel_id=1, source_target_pairs={{0,24},{8,0},{16,8},{24,16},{1,25},{9,1},{17,9},{25,17},{2,26},{10... | collective-permute-start | bytes 240008 | tf_op jit(solution)/shard_map/ppermute | solution.py:20
  110.1 45.4 %copy-start.2 = (bf16[1,200,200]{2,1,0:T(8,128)(2,1)}, bf16[1,200,200]{2,1,0:T(8,128)(2,1)S(1)}, u32[]{:S(2)}) copy-start(bf16[1,200,200]{2,1,0:T(8,128)(2,1)S(1)} %fusion.16.refs_1_) | copy-start | bytes 240004
  120.0 35.6 %all-to-all-start.1 = ((bf16[8,200,200]{2,1,0:T(8,128)(2,1)}), bf16[8,200,200]{2,1,0:T(8,128)(2,1)S(1)}, u32[]{:S(2)}, u32[]{:S(2)}) async-start(bf16[8,200,200]{2,1,0:T(8,128)(2,1)} %concatenate.38), calls=%async_computation.1 | async-start | bytes 1638400 | tf_op jit(solution)/shard_map/all_to_all | solution.py:67
  123.9 31.7 %collective-permute-start.21 = (bf16[4,200,200]{2,1,0:T(8,128)(2,1)}, bf16[4,200,200]{2,1,0:T(8,128)(2,1)}, u32[]{:S(2)}, u32[]{:S(2)}) collective-permute-start(bf16[4,200,200]{2,1,0:T(8,128)(2,1)} %constant_dynamic-update-slice_fusion.refs_6_), channel_id=1, source_target_pairs={{32,0},{64,32},{96,64},{128,96},{160,128},{192,160},{224,192},{33,... | collective-permute-start | bytes 960008 | tf_op jit(solution)/shard_map/ppermute | solution.py:26
  135.6 7.5 %collective-permute-start.17 = (bf16[1,200,200]{2,1,0:T(8,128)(2,1)S(1)}, bf16[1,200,200]{2,1,0:T(8,128)(2,1)S(1)}, u32[]{:S(2)}, u32[]{:S(2)}) collective-permute-start(bf16[1,200,200]{2,1,0:T(8,128)(2,1)S(1)} %fusion.16.refs_1_), channel_id=1, source_target_pairs={{0,8},{8,16},{16,24},{24,0},{1,9},{9,17},{17,25},{25,1},{2,10},{10... | collective-permute-start | bytes 240008 | tf_op jit(solution)/shard_map/ppermute | solution.py:20
  137.3 7.7 %collective-permute-start.18 = (bf16[1,200,200]{2,1,0:T(8,128)(2,1)S(1)}, bf16[1,200,200]{2,1,0:T(8,128)(2,1)S(1)}, u32[]{:S(2)}, u32[]{:S(2)}) collective-permute-start(bf16[1,200,200]{2,1,0:T(8,128)(2,1)S(1)} %fusion.16.refs_1_), channel_id=1, source_target_pairs={{0,16},{8,24},{16,0},{24,8},{1,17},{9,25},{17,1},{25,9},{2,18},{10... | collective-permute-start | bytes 240008 | tf_op jit(solution)/shard_map/ppermute | solution.py:20
  139.7 5.3 %collective-permute-start.19 = (bf16[1,200,200]{2,1,0:T(8,128)(2,1)S(1)}, bf16[1,200,200]{2,1,0:T(8,128)(2,1)S(1)}, u32[]{:S(2)}, u32[]{:S(2)}) collective-permute-start(bf16[1,200,200]{2,1,0:T(8,128)(2,1)S(1)} %fusion.16.refs_1_), channel_id=1, source_target_pairs={{0,24},{8,0},{16,8},{24,16},{1,25},{9,1},{17,9},{25,17},{2,26},{10... | collective-permute-start | bytes 240008 | tf_op jit(solution)/shard_map/ppermute | solution.py:20
  141.0 14.6 %collective-permute-start.25 = (bf16[4,200,200]{2,1,0:T(8,128)(2,1)S(1)}, bf16[4,200,200]{2,1,0:T(8,128)(2,1)}, u32[]{:S(2)}, u32[]{:S(2)}) collective-permute-start(bf16[4,200,200]{2,1,0:T(8,128)(2,1)S(1)} %pad_maximum_fusion.2), channel_id=1, source_target_pairs={{32,0},{64,32},{96,64},{128,96},{160,128},{192,160},{224,192},{33,... | collective-permute-start | bytes 960008 | tf_op jit(solution)/shard_map/ppermute | solution.py:26
  145.1 10.5 %collective-permute-start.20 = (bf16[4,200,200]{2,1,0:T(8,128)(2,1)S(1)}, bf16[4,200,200]{2,1,0:T(8,128)(2,1)}, u32[]{:S(2)}, u32[]{:S(2)}) collective-permute-start(bf16[4,200,200]{2,1,0:T(8,128)(2,1)S(1)} %pad_maximum_fusion.1), channel_id=1, source_target_pairs={{32,0},{64,32},{96,64},{128,96},{160,128},{192,160},{224,192},{33,... | collective-permute-start | bytes 960008 | tf_op jit(solution)/shard_map/ppermute | solution.py:26
  (25 other events, 400.6 us)
where the time goes:
time: 208 us; the launch traced here: 207 us
  starting transfers between devices  63.7 us (31%)
  blocking collectives  48.5 us (23%)
  waiting for transfers between devices  48.4 us (23%)
  Pallas kernels  26.4 us (13%)
  local copies, waits for them, and re-layouts  11.5 us (6%)
  other arithmetic  4.58 us (2%)
  matrix products  2.98 us (1%)
    ppermute x23, starting transfers between devices, moved(): lax.ppermute(block, axis, [(i, (i + distance) % count) for i in range(cou...  40.3 us
    ppermute x23, waiting for transfers between devices, moved(): lax.ppermute(block, axis, [(i, (i + distance) % count) for i in range(cou...  39.6 us
    pallas_call x1, Pallas kernels, dimer_energies(): pl.pallas_call(functools.partial(dimers_kernel, layout), in_specs=[pl.Blo...  20.4 us
    all_to_all x1, blocking collectives, exchanged(): return lax.all_to_all(array, axis, split_axis=0, concat_axis=0, tiled=True)  20 us
    all_to_all x1, blocking collectives, on_device(): lax.all_to_all(sent.reshape(members, 1, LANES), DEV, split_axis=0, concat...  16.8 us
    ppermute x3, starting transfers between devices, from_behind(): return lax.ppermute(block, axis, route)  16.2 us
    all_to_all x1, blocking collectives, sent_to_all(): return lax.all_to_all(copies, axis, split_axis=0, concat_axis=0, tiled=True)  11.7 us
    all_to_all x2, waiting for transfers between devices, exchanged(): return lax.all_to_all(array, axis, split_axis=0, concat_axis=0, tiled=True)  8.81 us
  transfers between devices with their start and end apart: 28, of which 11 were waited for; matrix products, arithmetic and copies ran while one was open for 6% of the time, Pallas kernels for 3%

commit v1 on v0

--- a/solution.py
+++ b/solution.py
@@ -232,7 +232,7 @@
             i = jnp.where(straight, word & 7, 8 + (word & 3))
             j = jnp.where(straight, lax.shift_right_logical(word, 3), lax.shift_right_logical(word, 2))
             operands.append(
-                (fock_ref[at(i)], dens_ref[i], ortho_ref[at(i)], fock_ref[at(j)], dens_ref[j], ortho_ref[at(j)])
+                (fock_ref[at(i)], dens_ref[i], ortho_ref[i], fock_ref[at(j)], dens_ref[j], ortho_ref[j])
             )
             target, slot = lax.shift_right_logical(place, 5), place & 31
             here = ((rows == target) & (columns == slot)) | (columns == lanes - 1)
@@ -304,7 +304,7 @@
         core_hamiltonian.astype(jnp.float32) + embedding.astype(jnp.float32) + coulomb
     ).astype(jnp.bfloat16)
 
-    ortho_row = exchanged(jnp.concatenate([orthogonalizers] * depth), "dev_1")
+    ortho_row = along_line(orthogonalizers, "dev_1")
     ortho_column = along_line(orthogonalizers, "dev_0")
     next_dens = from_behind(jnp.concatenate(dens_column), "grp", -1)
     next_ortho = from_behind(jnp.concatenate(ortho_column), "grp", -1)
@@ -337,7 +337,7 @@
         lists,
         parts(fock_row) + whole(fock_column) + parts(next_fock),
         whole(pieces + dens_column) + parts(next_dens),
-        parts(ortho_row) + whole(ortho_column) + parts(next_ortho),
+        whole(ortho_row + ortho_column) + parts(next_ortho),
         members,
     )
     arrived = lax.all_to_all(

time: 208 us -> 210 us (level)
  starting transfers between devices: 63.7 us -> 86.1 us
  blocking collectives: 48.5 us -> 27.5 us
  waiting for transfers between devices: 48.4 us -> 51.1 us
    all_to_all x1 -> x0, blocking collectives: 20 us -> none  [exchanged(): return lax.all_to_all(array, axis, split_axis=0, concat_axis=0, tiled=True)]
    ppermute x23 -> x30, starting transfers between devices: 40.3 us -> 59.1 us  [moved(): lax.ppermute(block, axis, [(i, (i + distance) % count) for i in range(cou...]
    ppermute x23 -> x30, waiting for transfers between devices: 39.6 us -> 45 us  [moved(): lax.ppermute(block, axis, [(i, (i + distance) % count) for i in range(cou...]
    ppermute x3, starting transfers between devices: 16.2 us -> 19.7 us  [from_behind(): return lax.ppermute(block, axis, route)]
    all_to_all x1, blocking collectives: 16.8 us -> 13.6 us  [on_device(): lax.all_to_all(sent.reshape(members, 1, LANES), DEV, split_axis=0, concat...]
    all_to_all x2, waiting for transfers between devices: 8.81 us -> 6.04 us  [exchanged(): return lax.all_to_all(array, axis, split_axis=0, concat_axis=0, tiled=True)]
    all_to_all x1, blocking collectives: 11.7 us -> 13.9 us  [sent_to_all(): return lax.all_to_all(copies, axis, split_axis=0, concat_axis=0, tiled=True)]
    unnamed x71 -> x81, local copies, waits for them, and re-layouts: 6.39 us -> 5.11 us
  transfers between devices with their start and end apart: 28 -> 35, of which waited for: 11 -> 13; matrix products, arithmetic and copies ran while one was open for 6% -> 5% of each run, Pallas kernels for 3% -> 3%
where the time goes in v1:
time: 210 us; the launch traced here: 209 us
  starting transfers between devices  86.1 us (41%)
  waiting for transfers between devices  51.1 us (24%)
  blocking collectives  27.5 us (13%)
  Pallas kernels  26.5 us (13%)
  local copies, waits for them, and re-layouts  9.41 us (4%)
  other arithmetic  4.61 us (2%)
  matrix products  2.98 us (1%)
    ppermute x30, starting transfers between devices, moved(): lax.ppermute(block, axis, [(i, (i + distance) % count) for i in range(cou...  59.1 us
    ppermute x30, waiting for transfers between devices, moved(): lax.ppermute(block, axis, [(i, (i + distance) % count) for i in range(cou...  45 us
    pallas_call x1, Pallas kernels, dimer_energies(): pl.pallas_call(functools.partial(dimers_kernel, layout), in_specs=[pl.Blo...  20.4 us
    ppermute x3, starting transfers between devices, from_behind(): return lax.ppermute(block, axis, route)  19.7 us
    all_to_all x1, blocking collectives, sent_to_all(): return lax.all_to_all(copies, axis, split_axis=0, concat_axis=0, tiled=True)  13.9 us
    all_to_all x1, blocking collectives, on_device(): lax.all_to_all(sent.reshape(members, 1, LANES), DEV, split_axis=0, concat...  13.6 us
    all_to_all x2, starting transfers between devices, exchanged(): return lax.all_to_all(array, axis, split_axis=0, concat_axis=0, tiled=True)  7.28 us
    pallas_call x1, Pallas kernels, dimer_lists(): pl.pallas_call(lists_kernel, in_specs=[smem] * 4, out_specs=smem, out_sha...  6.06 us
  transfers between devices with their start and end apart: 35, of which 13 were waited for; matrix products, arithmetic and copies ran while one was open for 5% of the time, Pallas kernels for 3%

profile of v1, /device:TPU:1, one launch (start us, length us, event | category | flops | bytes accessed | tf_op | source)
XLA Modules:
  0.0 209.5 jit_solution(11082746040131073809)
XLA Ops:
  2.8 2.5 %collective-permute-start.1 = (bf16[1,200,200]{2,1,0:T(8,128)(2,1)}, bf16[1,200,200]{2,1,0:T(8,128)(2,1)S(1)}, u32[]{:S(2)}, u32[]{:S(2)}) collective-permute-start(bf16[1,200,200]{2,1,0:T(8,128)(2,1)} %refs_14_.1), channel_id=1, source_target_pairs={{0,16},{8,24},{16,0},{24,8},{1,17},{9,25},{17,1},{25,9},{2,18},{10... | collective-permute-start | bytes 240008 | tf_op jit(solution)/shard_map/ppermute | solution.py:20
  7.3 2.3 %collective-permute-done.1.refs_16_ = bf16[1,200,200]{2,1,0:T(8,128)(2,1)S(1)} collective-permute-done((bf16[1,200,200]{2,1,0:T(8,128)(2,1)}, bf16[1,200,200]{2,1,0:T(8,128)(2,1)S(1)}, u32[]{:S(2)}, u32[]{:S(2)}) %collective-permute-start.1) | collective-permute-done | bytes 80032 | tf_op jit(solution)/shard_map/ppermute | solution.py:20
  9.7 5.9 %collective-permute-start.7 = (bf16[4,200,200]{2,1,0:T(8,128)(2,1)S(1)}, bf16[4,200,200]{2,1,0:T(8,128)(2,1)S(1)}, u32[]{:S(2)}, u32[]{:S(2)}) collective-permute-start(bf16[4,200,200]{2,1,0:T(8,128)(2,1)S(1)} %constant_dynamic-update-slice_fusion.refs_6_), channel_id=1, source_target_pairs={{0,7},{1,0},{2,1},{3,2},{4,3},{5,4},{6,5},{7,6},{8,15},{9,8},{10,9... | collective-permute-start | bytes 960008 | tf_op jit(solution)/shard_map/ppermute | solution.py:20
  15.6 7.2 %collective-permute-done.7.refs_13_ = bf16[4,200,200]{2,1,0:T(8,128)(2,1)S(1)} collective-permute-done((bf16[4,200,200]{2,1,0:T(8,128)(2,1)S(1)}, bf16[4,200,200]{2,1,0:T(8,128)(2,1)S(1)}, u32[]{:S(2)}, u32[]{:S(2)}) %collective-permute-start.7) | collective-permute-done | bytes 320032 | tf_op jit(solution)/shard_map/ppermute | solution.py:20
  22.8 3.4 %collective-permute-start.8 = (bf16[4,200,200]{2,1,0:T(8,128)(2,1)S(1)}, bf16[4,200,200]{2,1,0:T(8,128)(2,1)S(1)}, u32[]{:S(2)}, u32[]{:S(2)}) collective-permute-start(bf16[4,200,200]{2,1,0:T(8,128)(2,1)S(1)} %collective-permute-done.7.refs_13_), channel_id=1, source_target_pairs={{0,7},{1,0},{2,1},{3,2},{4,3},{5,4},{6,5},{7,6},{8,15},{9,8},{10,9... | collective-permute-start | bytes 960008 | tf_op jit(solution)/shard_map/ppermute | solution.py:20
  26.3 6.4 %collective-permute-done.8.refs_12_ = bf16[4,200,200]{2,1,0:T(8,128)(2,1)S(1)} collective-permute-done((bf16[4,200,200]{2,1,0:T(8,128)(2,1)S(1)}, bf16[4,200,200]{2,1,0:T(8,128)(2,1)S(1)}, u32[]{:S(2)}, u32[]{:S(2)}) %collective-permute-start.8) | collective-permute-done | bytes 320032 | tf_op jit(solution)/shard_map/ppermute | solution.py:20
  32.6 3.4 %collective-permute-start.9 = (bf16[4,200,200]{2,1,0:T(8,128)(2,1)S(1)}, bf16[4,200,200]{2,1,0:T(8,128)(2,1)S(1)}, u32[]{:S(2)}, u32[]{:S(2)}) collective-permute-start(bf16[4,200,200]{2,1,0:T(8,128)(2,1)S(1)} %collective-permute-done.8.refs_12_), channel_id=1, source_target_pairs={{0,7},{1,0},{2,1},{3,2},{4,3},{5,4},{6,5},{7,6},{8,15},{9,8},{10,9... | collective-permute-start | bytes 960008 | tf_op jit(solution)/shard_map/ppermute | solution.py:20
  36.2 5.4 %collective-permute-done.9.refs_11_ = bf16[4,200,200]{2,1,0:T(8,128)(2,1)S(1)} collective-permute-done((bf16[4,200,200]{2,1,0:T(8,128)(2,1)S(1)}, bf16[4,200,200]{2,1,0:T(8,128)(2,1)S(1)}, u32[]{:S(2)}, u32[]{:S(2)}) %collective-permute-start.9) | collective-permute-done | bytes 320032 | tf_op jit(solution)/shard_map/ppermute | solution.py:20
  42.9 2.1 %collective-permute-done.5.refs_9_ = bf16[4,200,200]{2,1,0:T(8,128)(2,1)S(1)} collective-permute-done((bf16[4,200,200]{2,1,0:T(8,128)(2,1)}, bf16[4,200,200]{2,1,0:T(8,128)(2,1)S(1)}, u32[]{:S(2)}, u32[]{:S(2)}) %collective-permute-start.5) | collective-permute-done | bytes 320032 | tf_op jit(solution)/shard_map/ppermute | solution.py:20
  45.1 2.7 %collective-permute-start.10 = (bf16[2,200,200]{2,1,0:T(8,128)(2,1)S(1)}, bf16[2,200,200]{2,1,0:T(8,128)(2,1)S(1)}, u32[]{:S(2)}, u32[]{:S(2)}) collective-permute-start(bf16[2,200,200]{2,1,0:T(8,128)(2,1)S(1)} %slice.74), channel_id=1, source_target_pairs={{0,7},{1,0},{2,1},{3,2},{4,3},{5,4},{6,5},{7,6},{8,15},{9,8},{10,9... | collective-permute-start | bytes 480008 | tf_op jit(solution)/shard_map/ppermute | solution.py:20
  53.8 2.7 %collective-permute-start.12 = (bf16[8,104,200]{2,0,1:T(8,128)(2,1)S(1)}, bf16[8,104,200]{2,0,1:T(8,128)(2,1)S(1)}, u32[]{:S(2)}, u32[]{:S(2)}) collective-permute-start(bf16[8,104,200]{2,0,1:T(8,128)(2,1)S(1)} %get-tuple-element.9), channel_id=1, source_target_pairs={{0,24},{8,0},{16,8},{24,16},{1,25},{9,1},{17,9},{25,17},{2,26},{10... | collective-permute-start | bytes 998408 | tf_op jit(solution)/shard_map/ppermute | solution.py:20
  56.5 2.7 %collective-permute-start.16 = (bf16[8,96,200]{2,0,1:T(8,128)(2,1)S(1)}, bf16[8,96,200]{2,0,1:T(8,128)(2,1)S(1)}, u32[]{:S(2)}, u32[]{:S(2)}) collective-permute-start(bf16[8,96,200]{2,0,1:T(8,128)(2,1)S(1)} %get-tuple-element.11), channel_id=1, source_target_pairs={{0,24},{8,0},{16,8},{24,16},{1,25},{9,1},{17,9},{25,17},{2,26},{10... | collective-permute-start | bytes 921608 | tf_op jit(solution)/shard_map/ppermute | solution.py:20
  59.2 2.3 %collective-permute-done.14 = bf16[8,96,200]{2,0,1:T(8,128)(2,1)S(1)} collective-permute-done((bf16[8,96,200]{2,0,1:T(8,128)(2,1)S(1)}, bf16[8,96,200]{2,0,1:T(8,128)(2,1)S(1)}, u32[]{:S(2)}, u32[]{:S(2)}) %collective-permute-start.14) | collective-permute-done | bytes 307232 | tf_op jit(solution)/shard_map/ppermute | solution.py:20
  61.9 3.0 %collective-permute-start.13 = (bf16[8,104,200]{2,0,1:T(8,128)(2,1)S(1)}, bf16[8,104,200]{2,0,1:T(8,128)(2,1)S(1)}, u32[]{:S(2)}, u32[]{:S(2)}) collective-permute-start(bf16[8,104,200]{2,0,1:T(8,128)(2,1)S(1)} %add_convert_fusion.1), channel_id=1, source_target_pairs={{0,24},{8,0},{16,8},{24,16},{1,25},{9,1},{17,9},{25,17},{2,26},{10... | collective-permute-start | bytes 998408 | tf_op jit(solution)/shard_map/ppermute | solution.py:20
  64.9 3.5 %collective-permute-done.16 = bf16[8,96,200]{2,0,1:T(8,128)(2,1)S(1)} collective-permute-done((bf16[8,96,200]{2,0,1:T(8,128)(2,1)S(1)}, bf16[8,96,200]{2,0,1:T(8,128)(2,1)S(1)}, u32[]{:S(2)}, u32[]{:S(2)}) %collective-permute-start.16) | collective-permute-done | bytes 307232 | tf_op jit(solution)/shard_map/ppermute | solution.py:20
  68.4 9.3 %collective-permute-done.15 = bf16[8,96,200]{2,0,1:T(8,128)(2,1)S(1)} collective-permute-done((bf16[8,96,200]{2,0,1:T(8,128)(2,1)S(1)}, bf16[8,96,200]{2,0,1:T(8,128)(2,1)S(1)}, u32[]{:S(2)}, u32[]{:S(2)}) %collective-permute-start.15) | collective-permute-done | bytes 307232 | tf_op jit(solution)/shard_map/ppermute | solution.py:20
  79.4 3.7 %all-to-all-start = ((bf16[8,200,200]{2,1,0:T(8,128)(2,1)}), bf16[8,200,200]{2,1,0:T(8,128)(2,1)S(1)}, u32[]{:S(2)}, u32[]{:S(2)}) async-start(bf16[8,200,200]{2,1,0:T(8,128)(2,1)} %copy.57), calls=%async_computation | async-start | bytes 1638400 | tf_op jit(solution)/shard_map/all_to_all | solution.py:67
  84.6 2.8 %collective-permute-start.30 = (bf16[1,200,200]{2,1,0:T(8,128)(2,1)S(1)}, bf16[1,200,200]{2,1,0:T(8,128)(2,1)S(1)}, u32[]{:S(2)}, u32[]{:S(2)}) collective-permute-start(bf16[1,200,200]{2,1,0:T(8,128)(2,1)S(1)} %copy-done.16), channel_id=1, source_target_pairs={{0,16},{8,24},{16,0},{24,8},{1,17},{9,25},{17,1},{25,9},{2,18},{10... | collective-permute-start | bytes 240008 | tf_op jit(solution)/shard_map/ppermute | solution.py:20
  92.8 6.0 %all-to-all-done = bf16[8,200,200]{2,1,0:T(8,128)(2,1)S(1)} async-done(((bf16[8,200,200]{2,1,0:T(8,128)(2,1)}), bf16[8,200,200]{2,1,0:T(8,128)(2,1)S(1)}, u32[]{:S(2)}, u32[]{:S(2)}) %all-to-all-start) | async-done | bytes 640032 | tf_op jit(solution)/shard_map/all_to_all | solution.py:67
  100.0 3.5 %all-to-all-start.1 = ((bf16[8,200,200]{2,1,0:T(8,128)(2,1)}), bf16[8,200,200]{2,1,0:T(8,128)(2,1)S(1)}, u32[]{:S(2)}, u32[]{:S(2)}) async-start(bf16[8,200,200]{2,1,0:T(8,128)(2,1)} %concatenate.35), calls=%async_computation.1 | async-start | bytes 1638400 | tf_op jit(solution)/shard_map/all_to_all | solution.py:67
  105.4 2.7 %collective-permute-start.18 = (bf16[1,200,200]{2,1,0:T(8,128)(2,1)S(1)}, bf16[1,200,200]{2,1,0:T(8,128)(2,1)S(1)}, u32[]{:S(2)}, u32[]{:S(2)}) collective-permute-start(bf16[1,200,200]{2,1,0:T(8,128)(2,1)S(1)} %fusion.16.refs_1_), channel_id=1, source_target_pairs={{0,16},{8,24},{16,0},{24,8},{1,17},{9,25},{17,1},{25,9},{2,18},{10... | collective-permute-start | bytes 240008 | tf_op jit(solution)/shard_map/ppermute | solution.py:20
  109.2 3.3 %collective-permute-start.24 = (bf16[1,200,200]{2,1,0:T(8,128)(2,1)S(1)}, bf16[1,200,200]{2,1,0:T(8,128)(2,1)}, u32[]{:S(2)}, u32[]{:S(2)}) collective-permute-start(bf16[1,200,200]{2,1,0:T(8,128)(2,1)S(1)} %copy-done.16), channel_id=1, source_target_pairs={{0,3},{1,4},{2,5},{3,6},{4,7},{5,0},{6,1},{7,2},{8,11},{9,12},{10,... | collective-permute-start | bytes 240008 | tf_op jit(solution)/shard_map/ppermute | solution.py:20
  112.6 15.9 %collective-permute-start.21 = (bf16[4,200,200]{2,1,0:T(8,128)(2,1)S(1)}, bf16[4,200,200]{2,1,0:T(8,128)(2,1)S(1)}, u32[]{:S(2)}, u32[]{:S(2)}) collective-permute-start(bf16[4,200,200]{2,1,0:T(8,128)(2,1)S(1)} %copy-done.27), channel_id=1, source_target_pairs={{32,0},{64,32},{96,64},{128,96},{160,128},{192,160},{224,192},{33,... | collective-permute-start | bytes 960008 | tf_op jit(solution)/shard_map/ppermute | solution.py:26
  133.9 4.1 %collective-permute-start.25 = (bf16[1,200,200]{2,1,0:T(8,128)(2,1)S(1)}, bf16[1,200,200]{2,1,0:T(8,128)(2,1)S(1)}, u32[]{:S(2)}, u32[]{:S(2)}) collective-permute-start(bf16[1,200,200]{2,1,0:T(8,128)(2,1)S(1)} %copy-done.16), channel_id=1, source_target_pairs={{0,4},{1,5},{2,6},{3,7},{4,0},{5,1},{6,2},{7,3},{8,12},{9,13},{10,... | collective-permute-start | bytes 240008 | tf_op jit(solution)/shard_map/ppermute | solution.py:20
  137.9 2.5 %collective-permute-start.26 = (bf16[1,200,200]{2,1,0:T(8,128)(2,1)S(1)}, bf16[1,200,200]{2,1,0:T(8,128)(2,1)S(1)}, u32[]{:S(2)}, u32[]{:S(2)}) collective-permute-start(bf16[1,200,200]{2,1,0:T(8,128)(2,1)S(1)} %copy-done.16), channel_id=1, source_target_pairs={{0,5},{1,6},{2,7},{3,0},{4,1},{5,2},{6,3},{7,4},{8,13},{9,14},{10,... | collective-permute-start | bytes 240008 | tf_op jit(solution)/shard_map/ppermute | solution.py:20
  142.8 2.9 %collective-permute-start.27 = (bf16[1,200,200]{2,1,0:T(8,128)(2,1)S(1)}, bf16[1,200,200]{2,1,0:T(8,128)(2,1)}, u32[]{:S(2)}, u32[]{:S(2)}) collective-permute-start(bf16[1,200,200]{2,1,0:T(8,128)(2,1)S(1)} %copy-done.16), channel_id=1, source_target_pairs={{0,6},{1,7},{2,0},{3,1},{4,2},{5,3},{6,4},{7,5},{8,14},{9,15},{10,... | collective-permute-start | bytes 240008 | tf_op jit(solution)/shard_map/ppermute | solution.py:20
  145.7 3.7 %collective-permute-done.26.refs_24_ = bf16[1,200,200]{2,1,0:T(8,128)(2,1)S(1)} collective-permute-done((bf16[1,200,200]{2,1,0:T(8,128)(2,1)S(1)}, bf16[1,200,200]{2,1,0:T(8,128)(2,1)S(1)}, u32[]{:S(2)}, u32[]{:S(2)}) %collective-permute-start.26) | collective-permute-done | bytes 80032 | tf_op jit(solution)/shard_map/ppermute | solution.py:20
  149.4 2.3 %collective-permute-start.28 = (bf16[1,200,200]{2,1,0:T(8,128)(2,1)S(1)}, bf16[1,200,200]{2,1,0:T(8,128)(2,1)}, u32[]{:S(2)}, u32[]{:S(2)}) collective-permute-start(bf16[1,200,200]{2,1,0:T(8,128)(2,1)S(1)} %copy-done.16), channel_id=1, source_target_pairs={{0,7},{1,0},{2,1},{3,2},{4,3},{5,4},{6,5},{7,6},{8,15},{9,8},{10,9... | collective-permute-start | bytes 240008 | tf_op jit(solution)/shard_map/ppermute | solution.py:20
  151.8 6.1 %dimer_lists.1.list_ref = s32[3,512]{1,0:T(4,128)} custom-call(s32[384]{0:T(512)} %get-tuple-element.13.choice_ref, s32[384]{0:T(512)} %get-tuple-element.12.slot_ref, s32[1]{0:T(128)} %bitcast.1.place_ref, s32[32]{0:T(128)} %select_reduce_fusion.1.load0_ref), custom_call_target="tpu_custom_call" | custom-call | flops 2000000000 | bytes 12288 | tf_op jit(solution)/shard_map/dimer_lists/pallas_call | solution.py:191
  159.6 20.4 %dimer_energies.1 = f32[32,128]{1,0:T(8,128)} custom-call(s32[3,512]{1,0:T(4,128)} %dimer_lists.1.list_ref, bf16[8,200,200]{2,1,0:T(8,128)(2,1)} %copy-done.5, bf16[1,200,200]{2,1,0:T(8,128)(2,1)} %copy-done.2, bf16[1,200,200]{2,1,0:T(8,128)(2,1)} %copy-done.20, bf16[1,200,200]{2,1,0:T(8,128)(2,1)} %copy-done.21, bf16[1,200,200]{2,1,0:T(8,128)(2,1)} %copy-done.22, ...), custom_call_target="tpu_custom_call" | custom-call | flops 5824000000 | bytes 3840000 | tf_op jit(solution)/shard_map/dimer_energies/pallas_call | solution.py:258
  180.1 13.6 %all_to_all.21 = f32[32,1,128]{2,1,0:T(1,128)S(1)} all-to-all(f32[32,1,128]{2,1,0:T(1,128)} %bitcast.27), channel_id=1, replica_groups=mesh['grp'=8,'dev_0'=4,'dev_1'=8] {'dev_0','dev_1'}, dimensions={0} | all-to-all | bytes 32768 | tf_op jit(solution)/shard_map/all_to_all | solution.py:343
  194.9 13.9 %all_to_all.22 = f32[8,1,1]{2,1,0:T(1,128)S(1)} all-to-all(f32[8,1,1]{2,1,0:T(1,128)S(1)} %broadcast_in_dim.51), channel_id=1, replica_groups=mesh['grp'=8,'dev_0'=4,'dev_1'=8] {'grp'}, dimensions={0} | all-to-all | bytes 64 | tf_op jit(solution)/shard_map/all_to_all | solution.py:72
  (160 shorter events, 35.8 us)
Async XLA Ops:
  0.7 6.6 %collective-permute-start = (bf16[1,200,200]{2,1,0:T(8,128)(2,1)}, bf16[1,200,200]{2,1,0:T(8,128)(2,1)S(1)}, u32[]{:S(2)}, u32[]{:S(2)}) collective-permute-start(bf16[1,200,200]{2,1,0:T(8,128)(2,1)} %refs_14_.1), channel_id=1, source_target_pairs={{0,8},{8,16},{16,24},{24,0},{1,9},{9,17},{17,25},{25,1},{2,10},{10... | collective-permute-start | bytes 240008 | tf_op jit(solution)/shard_map/ppermute | solution.py:20
  2.8 6.9 %collective-permute-start.1 = (bf16[1,200,200]{2,1,0:T(8,128)(2,1)}, bf16[1,200,200]{2,1,0:T(8,128)(2,1)S(1)}, u32[]{:S(2)}, u32[]{:S(2)}) collective-permute-start(bf16[1,200,200]{2,1,0:T(8,128)(2,1)} %refs_14_.1), channel_id=1, source_target_pairs={{0,16},{8,24},{16,0},{24,8},{1,17},{9,25},{17,1},{25,9},{2,18},{10... | collective-permute-start | bytes 240008 | tf_op jit(solution)/shard_map/ppermute | solution.py:20
  9.7 13.1 %collective-permute-start.7 = (bf16[4,200,200]{2,1,0:T(8,128)(2,1)S(1)}, bf16[4,200,200]{2,1,0:T(8,128)(2,1)S(1)}, u32[]{:S(2)}, u32[]{:S(2)}) collective-permute-start(bf16[4,200,200]{2,1,0:T(8,128)(2,1)S(1)} %constant_dynamic-update-slice_fusion.refs_6_), channel_id=1, source_target_pairs={{0,7},{1,0},{2,1},{3,2},{4,3},{5,4},{6,5},{7,6},{8,15},{9,8},{10,9... | collective-permute-start | bytes 960008 | tf_op jit(solution)/shard_map/ppermute | solution.py:20
  15.6 10.7 %collective-permute-start.3 = (bf16[4,200,200]{2,1,0:T(8,128)(2,1)S(1)}, bf16[4,200,200]{2,1,0:T(8,128)(2,1)S(1)}, u32[]{:S(2)}, u32[]{:S(2)}) collective-permute-start(bf16[4,200,200]{2,1,0:T(8,128)(2,1)S(1)} %constant_dynamic-update-slice_fusion.refs_6_), channel_id=1, source_target_pairs={{0,1},{1,2},{2,3},{3,4},{4,5},{5,6},{6,7},{7,0},{8,9},{9,10},{10,1... | collective-permute-start | bytes 960008 | tf_op jit(solution)/shard_map/ppermute | solution.py:20
  22.8 9.8 %collective-permute-start.8 = (bf16[4,200,200]{2,1,0:T(8,128)(2,1)S(1)}, bf16[4,200,200]{2,1,0:T(8,128)(2,1)S(1)}, u32[]{:S(2)}, u32[]{:S(2)}) collective-permute-start(bf16[4,200,200]{2,1,0:T(8,128)(2,1)S(1)} %collective-permute-done.7.refs_13_), channel_id=1, source_target_pairs={{0,7},{1,0},{2,1},{3,2},{4,3},{5,4},{6,5},{7,6},{8,15},{9,8},{10,9... | collective-permute-start | bytes 960008 | tf_op jit(solution)/shard_map/ppermute | solution.py:20
  26.2 9.8 %collective-permute-start.4 = (bf16[4,200,200]{2,1,0:T(8,128)(2,1)S(1)}, bf16[4,200,200]{2,1,0:T(8,128)(2,1)}, u32[]{:S(2)}, u32[]{:S(2)}) collective-permute-start(bf16[4,200,200]{2,1,0:T(8,128)(2,1)S(1)} %collective-permute-done.3.refs_7_), channel_id=1, source_target_pairs={{0,1},{1,2},{2,3},{3,4},{4,5},{5,6},{6,7},{7,0},{8,9},{9,10},{10,1... | collective-permute-start | bytes 960008 | tf_op jit(solution)/shard_map/ppermute | solution.py:20
  32.6 8.9 %collective-permute-start.9 = (bf16[4,200,200]{2,1,0:T(8,128)(2,1)S(1)}, bf16[4,200,200]{2,1,0:T(8,128)(2,1)S(1)}, u32[]{:S(2)}, u32[]{:S(2)}) collective-permute-start(bf16[4,200,200]{2,1,0:T(8,128)(2,1)S(1)} %collective-permute-done.8.refs_12_), channel_id=1, source_target_pairs={{0,7},{1,0},{2,1},{3,2},{4,3},{5,4},{6,5},{7,6},{8,15},{9,8},{10,9... | collective-permute-start | bytes 960008 | tf_op jit(solution)/shard_map/ppermute | solution.py:20
  36.1 9.0 %collective-permute-start.5 = (bf16[4,200,200]{2,1,0:T(8,128)(2,1)}, bf16[4,200,200]{2,1,0:T(8,128)(2,1)S(1)}, u32[]{:S(2)}, u32[]{:S(2)}) collective-permute-start(bf16[4,200,200]{2,1,0:T(8,128)(2,1)} %collective-permute-done.4.refs_8_), channel_id=1, source_target_pairs={{0,1},{1,2},{2,3},{3,4},{4,5},{5,6},{6,7},{7,0},{8,9},{9,10},{10,1... | collective-permute-start | bytes 960008 | tf_op jit(solution)/shard_map/ppermute | solution.py:20
  45.0 5.9 %collective-permute-start.6 = (bf16[2,200,200]{2,1,0:T(8,128)(2,1)S(1)}, bf16[2,200,200]{2,1,0:T(8,128)(2,1)S(1)}, u32[]{:S(2)}, u32[]{:S(2)}) collective-permute-start(bf16[2,200,200]{2,1,0:T(8,128)(2,1)S(1)} %slice.73), channel_id=1, source_target_pairs={{0,1},{1,2},{2,3},{3,4},{4,5},{5,6},{6,7},{7,0},{8,9},{9,10},{10,1... | collective-permute-start | bytes 480008 | tf_op jit(solution)/shard_map/ppermute | solution.py:20
  53.2 8.3 %collective-permute-start.14 = (bf16[8,96,200]{2,0,1:T(8,128)(2,1)S(1)}, bf16[8,96,200]{2,0,1:T(8,128)(2,1)S(1)}, u32[]{:S(2)}, u32[]{:S(2)}) collective-permute-start(bf16[8,96,200]{2,0,1:T(8,128)(2,1)S(1)} %get-tuple-element.10), channel_id=1, source_target_pairs={{0,8},{8,16},{16,24},{24,0},{1,9},{9,17},{17,25},{25,1},{2,10},{10... | collective-permute-start | bytes 921608 | tf_op jit(solution)/shard_map/ppermute | solution.py:20
  53.8 8.0 %collective-permute-start.12 = (bf16[8,104,200]{2,0,1:T(8,128)(2,1)S(1)}, bf16[8,104,200]{2,0,1:T(8,128)(2,1)S(1)}, u32[]{:S(2)}, u32[]{:S(2)}) collective-permute-start(bf16[8,104,200]{2,0,1:T(8,128)(2,1)S(1)} %get-tuple-element.9), channel_id=1, source_target_pairs={{0,24},{8,0},{16,8},{24,16},{1,25},{9,1},{17,9},{25,17},{2,26},{10... | collective-permute-start | bytes 998408 | tf_op jit(solution)/shard_map/ppermute | solution.py:20
  56.5 21.4 %collective-permute-start.11 = (bf16[8,104,200]{2,0,1:T(8,128)(2,1)S(1)}, bf16[8,104,200]{2,0,1:T(8,128)(2,1)S(1)}, u32[]{:S(2)}, u32[]{:S(2)}) collective-permute-start(bf16[8,104,200]{2,0,1:T(8,128)(2,1)S(1)} %get-tuple-element.8), channel_id=1, source_target_pairs={{0,8},{8,16},{16,24},{24,0},{1,9},{9,17},{17,25},{25,1},{2,10},{10... | collective-permute-start | bytes 998408 | tf_op jit(solution)/shard_map/ppermute | solution.py:20
  56.5 12.0 %collective-permute-start.16 = (bf16[8,96,200]{2,0,1:T(8,128)(2,1)S(1)}, bf16[8,96,200]{2,0,1:T(8,128)(2,1)S(1)}, u32[]{:S(2)}, u32[]{:S(2)}) collective-permute-start(bf16[8,96,200]{2,0,1:T(8,128)(2,1)S(1)} %get-tuple-element.11), channel_id=1, source_target_pairs={{0,24},{8,0},{16,8},{24,16},{1,25},{9,1},{17,9},{25,17},{2,26},{10... | collective-permute-start | bytes 921608 | tf_op jit(solution)/shard_map/ppermute | solution.py:20
  61.7 16.1 %collective-permute-start.15 = (bf16[8,96,200]{2,0,1:T(8,128)(2,1)S(1)}, bf16[8,96,200]{2,0,1:T(8,128)(2,1)S(1)}, u32[]{:S(2)}, u32[]{:S(2)}) collective-permute-start(bf16[8,96,200]{2,0,1:T(8,128)(2,1)S(1)} %add_convert_fusion.3), channel_id=1, source_target_pairs={{0,8},{8,16},{16,24},{24,0},{1,9},{9,17},{17,25},{25,1},{2,10},{10... | collective-permute-start | bytes 921608 | tf_op jit(solution)/shard_map/ppermute | solution.py:20
  61.9 16.0 %collective-permute-start.13 = (bf16[8,104,200]{2,0,1:T(8,128)(2,1)S(1)}, bf16[8,104,200]{2,0,1:T(8,128)(2,1)S(1)}, u32[]{:S(2)}, u32[]{:S(2)}) collective-permute-start(bf16[8,104,200]{2,0,1:T(8,128)(2,1)S(1)} %add_convert_fusion.1), channel_id=1, source_target_pairs={{0,24},{8,0},{16,8},{24,16},{1,25},{9,1},{17,9},{25,17},{2,26},{10... | collective-permute-start | bytes 998408 | tf_op jit(solution)/shard_map/ppermute | solution.py:20
  79.4 19.5 %all-to-all-start = ((bf16[8,200,200]{2,1,0:T(8,128)(2,1)}), bf16[8,200,200]{2,1,0:T(8,128)(2,1)S(1)}, u32[]{:S(2)}, u32[]{:S(2)}) async-start(bf16[8,200,200]{2,1,0:T(8,128)(2,1)} %copy.57), calls=%async_computation | async-start | bytes 1638400 | tf_op jit(solution)/shard_map/all_to_all | solution.py:67
  83.1 20.8 %collective-permute-start.29 = (bf16[1,200,200]{2,1,0:T(8,128)(2,1)S(1)}, bf16[1,200,200]{2,1,0:T(8,128)(2,1)S(1)}, u32[]{:S(2)}, u32[]{:S(2)}) collective-permute-start(bf16[1,200,200]{2,1,0:T(8,128)(2,1)S(1)} %copy-done.16), channel_id=1, source_target_pairs={{0,8},{8,16},{16,24},{24,0},{1,9},{9,17},{17,25},{25,1},{2,10},{10... | collective-permute-start | bytes 240008 | tf_op jit(solution)/shard_map/ppermute | solution.py:20
  84.6 20.8 %collective-permute-start.30 = (bf16[1,200,200]{2,1,0:T(8,128)(2,1)S(1)}, bf16[1,200,200]{2,1,0:T(8,128)(2,1)S(1)}, u32[]{:S(2)}, u32[]{:S(2)}) collective-permute-start(bf16[1,200,200]{2,1,0:T(8,128)(2,1)S(1)} %copy-done.16), channel_id=1, source_target_pairs={{0,16},{8,24},{16,0},{24,8},{1,17},{9,25},{17,1},{25,9},{2,18},{10... | collective-permute-start | bytes 240008 | tf_op jit(solution)/shard_map/ppermute | solution.py:20
  87.4 20.6 %collective-permute-start.31 = (bf16[1,200,200]{2,1,0:T(8,128)(2,1)S(1)}, bf16[1,200,200]{2,1,0:T(8,128)(2,1)S(1)}, u32[]{:S(2)}, u32[]{:S(2)}) collective-permute-start(bf16[1,200,200]{2,1,0:T(8,128)(2,1)S(1)} %copy-done.16), channel_id=1, source_target_pairs={{0,24},{8,0},{16,8},{24,16},{1,25},{9,1},{17,9},{25,17},{2,26},{10... | collective-permute-start | bytes 240008 | tf_op jit(solution)/shard_map/ppermute | solution.py:20
  88.2 42.3 %collective-permute-start.22 = (bf16[1,200,200]{2,1,0:T(8,128)(2,1)S(1)}, bf16[1,200,200]{2,1,0:T(8,128)(2,1)S(1)}, u32[]{:S(2)}, u32[]{:S(2)}) collective-permute-start(bf16[1,200,200]{2,1,0:T(8,128)(2,1)S(1)} %copy-done.16), channel_id=1, source_target_pairs={{0,1},{1,2},{2,3},{3,4},{4,5},{5,6},{6,7},{7,0},{8,9},{9,10},{10,1... | collective-permute-start | bytes 240008 | tf_op jit(solution)/shard_map/ppermute | solution.py:20
  89.7 44.2 %collective-permute-start.23 = (bf16[1,200,200]{2,1,0:T(8,128)(2,1)S(1)}, bf16[1,200,200]{2,1,0:T(8,128)(2,1)}, u32[]{:S(2)}, u32[]{:S(2)}) collective-permute-start(bf16[1,200,200]{2,1,0:T(8,128)(2,1)S(1)} %copy-done.16), channel_id=1, source_target_pairs={{0,2},{1,3},{2,4},{3,5},{4,6},{5,7},{6,0},{7,1},{8,10},{9,11},{10,... | collective-permute-start | bytes 240008 | tf_op jit(solution)/shard_map/ppermute | solution.py:20
  100.0 58.7 %all-to-all-start.1 = ((bf16[8,200,200]{2,1,0:T(8,128)(2,1)}), bf16[8,200,200]{2,1,0:T(8,128)(2,1)S(1)}, u32[]{:S(2)}, u32[]{:S(2)}) async-start(bf16[8,200,200]{2,1,0:T(8,128)(2,1)} %concatenate.35), calls=%async_computation.1 | async-start | bytes 1638400 | tf_op jit(solution)/shard_map/all_to_all | solution.py:67
  105.4 7.2 %collective-permute-start.18 = (bf16[1,200,200]{2,1,0:T(8,128)(2,1)S(1)}, bf16[1,200,200]{2,1,0:T(8,128)(2,1)S(1)}, u32[]{:S(2)}, u32[]{:S(2)}) collective-permute-start(bf16[1,200,200]{2,1,0:T(8,128)(2,1)S(1)} %fusion.16.refs_1_), channel_id=1, source_target_pairs={{0,16},{8,24},{16,0},{24,8},{1,17},{9,25},{17,1},{25,9},{2,18},{10... | collective-permute-start | bytes 240008 | tf_op jit(solution)/shard_map/ppermute | solution.py:20
  108.1 20.4 %collective-permute-start.19 = (bf16[1,200,200]{2,1,0:T(8,128)(2,1)S(1)}, bf16[1,200,200]{2,1,0:T(8,128)(2,1)S(1)}, u32[]{:S(2)}, u32[]{:S(2)}) collective-permute-start(bf16[1,200,200]{2,1,0:T(8,128)(2,1)S(1)} %fusion.16.refs_1_), channel_id=1, source_target_pairs={{0,24},{8,0},{16,8},{24,16},{1,25},{9,1},{17,9},{25,17},{2,26},{10... | collective-permute-start | bytes 240008 | tf_op jit(solution)/shard_map/ppermute | solution.py:20
  109.2 28.7 %collective-permute-start.24 = (bf16[1,200,200]{2,1,0:T(8,128)(2,1)S(1)}, bf16[1,200,200]{2,1,0:T(8,128)(2,1)}, u32[]{:S(2)}, u32[]{:S(2)}) collective-permute-start(bf16[1,200,200]{2,1,0:T(8,128)(2,1)S(1)} %copy-done.16), channel_id=1, source_target_pairs={{0,3},{1,4},{2,5},{3,6},{4,7},{5,0},{6,1},{7,2},{8,11},{9,12},{10,... | collective-permute-start | bytes 240008 | tf_op jit(solution)/shard_map/ppermute | solution.py:20
  112.6 45.4 %collective-permute-start.21 = (bf16[4,200,200]{2,1,0:T(8,128)(2,1)S(1)}, bf16[4,200,200]{2,1,0:T(8,128)(2,1)S(1)}, u32[]{:S(2)}, u32[]{:S(2)}) collective-permute-start(bf16[4,200,200]{2,1,0:T(8,128)(2,1)S(1)} %copy-done.27), channel_id=1, source_target_pairs={{32,0},{64,32},{96,64},{128,96},{160,128},{192,160},{224,192},{33,... | collective-permute-start | bytes 960008 | tf_op jit(solution)/shard_map/ppermute | solution.py:26
  128.5 29.5 %collective-permute-start.32 = (bf16[4,200,200]{2,1,0:T(8,128)(2,1)S(1)}, bf16[4,200,200]{2,1,0:T(8,128)(2,1)}, u32[]{:S(2)}, u32[]{:S(2)}) collective-permute-start(bf16[4,200,200]{2,1,0:T(8,128)(2,1)S(1)} %pad_maximum_fusion.2), channel_id=1, source_target_pairs={{32,0},{64,32},{96,64},{128,96},{160,128},{192,160},{224,192},{33,... | collective-permute-start | bytes 960008 | tf_op jit(solution)/shard_map/ppermute | solution.py:26
  130.5 27.4 %collective-permute-start.20 = (bf16[4,200,200]{2,1,0:T(8,128)(2,1)S(1)}, bf16[4,200,200]{2,1,0:T(8,128)(2,1)}, u32[]{:S(2)}, u32[]{:S(2)}) collective-permute-start(bf16[4,200,200]{2,1,0:T(8,128)(2,1)S(1)} %pad_maximum_fusion.1), channel_id=1, source_target_pairs={{32,0},{64,32},{96,64},{128,96},{160,128},{192,160},{224,192},{33,... | collective-permute-start | bytes 960008 | tf_op jit(solution)/shard_map/ppermute | solution.py:26
  133.9 9.0 %collective-permute-start.25 = (bf16[1,200,200]{2,1,0:T(8,128)(2,1)S(1)}, bf16[1,200,200]{2,1,0:T(8,128)(2,1)S(1)}, u32[]{:S(2)}, u32[]{:S(2)}) collective-permute-start(bf16[1,200,200]{2,1,0:T(8,128)(2,1)S(1)} %copy-done.16), channel_id=1, source_target_pairs={{0,4},{1,5},{2,6},{3,7},{4,0},{5,1},{6,2},{7,3},{8,12},{9,13},{10,... | collective-permute-start | bytes 240008 | tf_op jit(solution)/shard_map/ppermute | solution.py:20
  137.9 11.5 %collective-permute-start.26 = (bf16[1,200,200]{2,1,0:T(8,128)(2,1)S(1)}, bf16[1,200,200]{2,1,0:T(8,128)(2,1)S(1)}, u32[]{:S(2)}, u32[]{:S(2)}) collective-permute-start(bf16[1,200,200]{2,1,0:T(8,128)(2,1)S(1)} %copy-done.16), channel_id=1, source_target_pairs={{0,5},{1,6},{2,7},{3,0},{4,1},{5,2},{6,3},{7,4},{8,13},{9,14},{10,... | collective-permute-start | bytes 240008 | tf_op jit(solution)/shard_map/ppermute | solution.py:20
  142.8 15.1 %collective-permute-start.27 = (bf16[1,200,200]{2,1,0:T(8,128)(2,1)S(1)}, bf16[1,200,200]{2,1,0:T(8,128)(2,1)}, u32[]{:S(2)}, u32[]{:S(2)}) collective-permute-start(bf16[1,200,200]{2,1,0:T(8,128)(2,1)S(1)} %copy-done.16), channel_id=1, source_target_pairs={{0,6},{1,7},{2,0},{3,1},{4,2},{5,3},{6,4},{7,5},{8,14},{9,15},{10,... | collective-permute-start | bytes 240008 | tf_op jit(solution)/shard_map/ppermute | solution.py:20
  149.4 8.5 %collective-permute-start.28 = (bf16[1,200,200]{2,1,0:T(8,128)(2,1)S(1)}, bf16[1,200,200]{2,1,0:T(8,128)(2,1)}, u32[]{:S(2)}, u32[]{:S(2)}) collective-permute-start(bf16[1,200,200]{2,1,0:T(8,128)(2,1)S(1)} %copy-done.16), channel_id=1, source_target_pairs={{0,7},{1,0},{2,1},{3,2},{4,3},{5,4},{6,5},{7,6},{8,15},{9,8},{10,9... | collective-permute-start | bytes 240008 | tf_op jit(solution)/shard_map/ppermute | solution.py:20
  (37 other events, 848.2 us)
